TPU v7x, 256 devices: a whole 4x4x8 slice. The times are simulated.
256 devices in a mesh: fsdp: 64 (over z, y, core), rep: 4 (over x).
Axes of the slice: x: 4, y: 4, z: 8, core: 2. Of those that a mesh axis runs over, the one named last changes fastest.
Arguments:
- partial_grad: bfloat16 [4, 64, 1024, 1024], P('rep', None, 'fsdp'), may hold values from -3 to 3
- owner_table: int32 [64, 2], replicated, may hold values from -1 to 63, as said below
- left_stat: float32 [64, 2, 1024, 1024], P('fsdp', None, None, 'rep'), may hold values from -6 to 6
- right_stat: float32 [64, 2, 1024, 1024], P('fsdp', None, None, 'rep'), may hold values from -6 to 6
- left_root: bfloat16 [64, 2, 1024, 1024], P('fsdp', None, None, 'rep'), may hold values from -0.1875 to 0.1875
- right_root: bfloat16 [64, 2, 1024, 1024], P('fsdp', None, None, 'rep'), may hold values from -0.1875 to 0.1875
Outputs:
- left_new: float32 [64, 2, 1024, 1024], P('fsdp', None, None, 'rep')
- right_new: float32 [64, 2, 1024, 1024], P('fsdp', None, None, 'rep')
- update: bfloat16 [64, 1024, 1024], P(None, 'fsdp', 'rep')
Inputs may be any that keep to these rules, and one draw needn't show every extreme that they name: `owner_table`: each of the 64 blocks stands in exactly one slot and -1 marks an empty slot; some owner fills all 2 slots and some owner has none.
All inputs are finite; a program needn't handle non-finite values.
Results may differ from a plain program's by a relative error of at most 0.014.
Values may be sent and summed in bfloat16 or wider, within the bound.
A program may use at most 64 MiB of HBM per device.

v0:
```python
import jax
import jax.numpy as jnp
from jax import lax
from jax.sharding import PartitionSpec as P

decay_rate = 0.99


def in_blocks(x, dim, size):
    shape = x.shape
    parts = x.reshape(*shape[:dim], size, shape[dim] // size, *shape[dim + 1 :])
    return jnp.moveaxis(parts, dim, 0)


def summed_on_arrival(x, axis, dim):
    size = lax.axis_size(axis)
    parts = lax.all_to_all(in_blocks(x, dim, size), axis, 0, 0, tiled=True)
    return jnp.sum(parts.astype(jnp.float32), axis=0)


def on_device(partial_grad, owner_table, left_stat, right_stat, left_root, right_root):
    local_grad = partial_grad[0]
    block_count = local_grad.shape[0]
    my_row = lax.dynamic_index_in_dim(owner_table, lax.axis_index("fsdp"), 0, keepdims=False)
    is_filled = my_row >= 0
    sender_index = jnp.maximum(owner_table.T, 0)
    sender_mask = owner_table.T >= 0
    shares = summed_on_arrival(
        local_grad.astype(jnp.float32).astype(jnp.bfloat16), "rep", 2
    ).astype(jnp.bfloat16)
    picked = jnp.take(shares, sender_index, axis=0)
    picked = jnp.where(sender_mask[:, :, None, None], picked, jnp.zeros((), picked.dtype))
    columns = lax.all_to_all(
        picked.reshape(picked.shape[0], -1, picked.shape[3]),
        "fsdp",
        split_axis=1,
        concat_axis=1,
        tiled=True,
    )
    gradient = lax.all_gather(columns, "rep", axis=2, tiled=True)
    share_width = left_stat.shape[3]
    first_col = lax.axis_index("rep") * share_width
    rows_share = lax.dynamic_slice_in_dim(gradient, first_col, share_width, 1)
    cols_share = lax.dynamic_slice_in_dim(gradient, first_col, share_width, 2)
    left_term = jnp.einsum("sik,sjk->sij", gradient, rows_share, preferred_element_type=jnp.float32)
    right_term = jnp.einsum(
        "ski,skj->sij", gradient, cols_share, preferred_element_type=jnp.float32
    )
    keeper = is_filled[:, None, None]
    left_next = jnp.where(
        keeper, decay_rate * left_stat[0] + (1.0 - decay_rate) * left_term, left_stat[0]
    )
    right_next = jnp.where(
        keeper, decay_rate * right_stat[0] + (1.0 - decay_rate) * right_term, right_stat[0]
    )
    applied = jnp.einsum(
        "sik,skj->sij",
        lax.all_gather(left_root[0], "rep", axis=2, tiled=True),
        gradient,
        preferred_element_type=jnp.float32,
    ).astype(jnp.bfloat16)
    result_cols = jnp.einsum(
        "sik,skj->sij", applied, right_root[0], preferred_element_type=jnp.float32
    ).astype(jnp.bfloat16)
    returned = lax.all_to_all(result_cols, "fsdp", split_axis=1, concat_axis=0, tiled=True)
    flat_table = owner_table.reshape(-1)
    slot_ids = jnp.arange(flat_table.shape[0], dtype=jnp.int32)
    block_ids = jnp.arange(block_count, dtype=jnp.int32)
    positions = jnp.sum(
        jnp.where(flat_table[None, :] == block_ids[:, None], slot_ids[None, :], 0), axis=1
    )
    update = jnp.take(returned, positions, axis=0)
    return (left_next[None], right_next[None], update)


def solution(mesh):
    return jax.shard_map(
        on_device,
        mesh=mesh,
        in_specs=(
            P("rep", None, "fsdp", None),
            P(),
            P("fsdp", None, None, "rep"),
            P("fsdp", None, None, "rep"),
            P("fsdp", None, None, "rep"),
            P("fsdp", None, None, "rep"),
        ),
        out_specs=(
            P("fsdp", None, None, "rep"),
            P("fsdp", None, None, "rep"),
            P(None, "fsdp", "rep"),
        ),
        check_vma=False,
    )
```

profile of v0, /device:TPU:1, one launch (start us, length us, event | category | flops | bytes accessed | tf_op | source)
XLA Modules:
  0.0 213.5 jit_solution(4872526677755833323)
XLA Ops:
  7.2 0.7 all-gather.6.cloned.1.call-update
  7.9 3.3 %reshape.46 = bf16[64,16,4,256]{3,2,1,0:T(4,128)(2,1)S(1)} reshape(bf16[1,64,16,1024]{3,2,1,0:T(8,128)(2,1)} %param.6) | data formatting | bytes 4194304 | tf_op jit(solution)/shard_map/reshape | solution.py:11
  11.3 1.6 copy.32
  12.9 5.0 %all-to-all-start = ((bf16[4,64,16,256]{3,2,1,0:T(8,128)(2,1)}), bf16[4,64,16,256]{3,2,1,0:T(8,128)(2,1)S(1)}, u32[]{:S(2)}, u32[]{:S(2)}) async-start(bf16[4,64,16,256]{3,2,1,0:T(8,128)(2,1)} %copy.32), calls=%async_computation | async-start | bytes 4194304 | tf_op jit(solution)/shard_map/all_to_all | solution.py:17
  18.4 35.2 %all-to-all-done = bf16[4,64,16,256]{3,2,1,0:T(8,128)(2,1)S(1)} async-done(((bf16[4,64,16,256]{3,2,1,0:T(8,128)(2,1)}), bf16[4,64,16,256]{3,2,1,0:T(8,128)(2,1)S(1)}, u32[]{:S(2)}, u32[]{:S(2)}) %all-to-all-start) | async-done | bytes 2097184 | tf_op jit(solution)/shard_map/all_to_all | solution.py:17
  53.5 1.2 reduce_sum.23
  54.8 1.7 gather_fusion
  56.5 0.9 fusion.18
  57.4 1.1 copy.33
  58.5 42.5 %all_to_all.28 = bf16[2,1024,256]{2,0,1:T(2,128)(2,1)S(1)} all-to-all(bf16[2,1024,256]{2,0,1:T(2,128)(2,1)S(1)} %copy.33), channel_id=1, replica_groups=mesh['fsdp'=64,'rep'=4] {'fsdp'}, dimensions={1} | all-to-all | bytes 2097152 | tf_op jit(solution)/shard_map/all_to_all | solution.py:33
  101.0 1.1 copy.34
  102.2 50.5 %all-gather.4.cloned.1.call-done = bf16[2,1024,1024]{2,1,0:T(8,128)(2,1)} async-done(((bf16[2,1024,256]{2,1,0:T(8,128)(2,1)}), bf16[2,1024,1024]{2,1,0:T(8,128)(2,1)}) %all-gather.4.cloned.1.call-update) | async-done | bytes 4194320 | tf_op jit(solution)/shard_map/all_gather | solution.py:40
  152.7 9.9 %fusion.12 = bf16[2,1024,256]{2,1,0:T(8,128)(2,1)S(1)} fusion(bf16[2,1024,1024]{2,1,0:T(8,128)(2,1)} %all-gather.4.cloned.1.call-done, bf16[1,2,1024,1024]{3,2,1,0:T(8,128)(2,1)} %all-gather.6.cloned.1.call-done, bf16[1,2,1024,256]{3,2,1,0:T(8,128)(2,1)S(1)} %copy-done), kind=kOutput, calls=%fused_computation.14 | convolution fusion | flops 5371330560 | bytes 10485760 | tf_op jit(solution)/shard_map/sik,skj->sij/dot_general | solution.py:62
  162.5 2.1 copy.39
  164.6 12.1 %all-to-all-start.2 = ((bf16[2,1024,256]{2,0,1:T(2,128)(2,1)}), bf16[2,1024,256]{2,0,1:T(2,128)(2,1)S(1)}, u32[]{:S(2)}, u32[]{:S(2)}) async-start(bf16[2,1024,256]{2,0,1:T(2,128)(2,1)} %copy.39), calls=%async_computation.2 | async-start | bytes 2097152 | tf_op jit(solution)/shard_map/all_to_all | solution.py:65
  176.8 0.1 eq.15
  176.9 0.2 compare_reduce_fusion
  177.3 6.4 %fusion.5 = f32[1,2,1024,256]{3,2,1,0:T(8,128)} fusion(f32[1,2,1024,256]{3,2,1,0:T(8,128)} %param.9, bf16[2,1024,1024]{2,1,0:T(8,128)(2,1)} %all-gather.4.cloned.1.call-done, s32[]{:T(128)S(6)} %select_n.55, pred[2]{0:T(512)(128)(4,1)S(1)} %compare_reduce_fusion), kind=kOutput, calls=%fused_computation.9 | convolution fusion | flops 1075838976 | bytes 9437190 | tf_op jit(solution)/shard_map/ski,skj->sij/dot_general | solution.py:46
  183.7 2.7 %fusion.7 = f32[1,2,1024,256]{3,2,1,0:T(8,128)} fusion(f32[1,2,1024,256]{3,2,1,0:T(8,128)S(1)} %copy-done.3, bf16[2,1024,1024]{2,1,0:T(8,128)(2,1)S(1)} %copy-done.2, s32[]{:T(128)S(6)} %select_n.55, pred[2]{0:T(512)(128)(4,1)S(1)} %compare_reduce_fusion), kind=kOutput, calls=%fused_computation.13 | convolution fusion | flops 1075838976 | bytes 9437700 | tf_op jit(solution)/shard_map/sik,sjk->sij/dot_general | solution.py:45
  186.5 18.4 %all-to-all-done.2 = bf16[2,1024,256]{2,0,1:T(2,128)(2,1)S(1)} async-done(((bf16[2,1024,256]{2,0,1:T(2,128)(2,1)}), bf16[2,1024,256]{2,0,1:T(2,128)(2,1)S(1)}, u32[]{:S(2)}, u32[]{:S(2)}) %all-to-all-start.2) | async-done | bytes 1048608 | tf_op jit(solution)/shard_map/all_to_all | solution.py:65
  204.8 0.1 copy.40
  205.0 0.1 copy.41
  205.1 0.6 gather_fusion.1
  205.7 0.9 broadcast_select_fusion
  (26 shorter events, 0.8 us)
Async XLA Ops:
  7.2 145.5 %copy-start = (bf16[1,2,1024,256]{3,2,1,0:T(8,128)(2,1)S(1)}, bf16[1,2,1024,256]{3,2,1,0:T(8,128)(2,1)}, u32[]{:S(2)}) copy-start(bf16[1,2,1024,256]{3,2,1,0:T(8,128)(2,1)} %param.11) | copy-start | bytes 3145732
  7.2 95.0 %all-gather.6.cloned.1.call-start = ((), (), s32[]{:S(2)}) async-start(), calls=%async_computation.4 | async-start | bytes 5242880 | tf_op jit(solution)/shard_map/all_gather | solution.py:58
  12.9 5.0 %copy-start.1 = (s32[64,2]{0,1:T(2,128)S(1)}, s32[64,2]{0,1:T(2,128)}, u32[]{:S(2)}) copy-start(s32[64,2]{0,1:T(2,128)} %param.7) | copy-start | bytes 1540
  12.9 40.7 %all-to-all-start = ((bf16[4,64,16,256]{3,2,1,0:T(8,128)(2,1)}), bf16[4,64,16,256]{3,2,1,0:T(8,128)(2,1)S(1)}, u32[]{:S(2)}, u32[]{:S(2)}) async-start(bf16[4,64,16,256]{3,2,1,0:T(8,128)(2,1)} %copy.32), calls=%async_computation | async-start | bytes 4194304 | tf_op jit(solution)/shard_map/all_to_all | solution.py:17
  17.8 134.8 %all-gather.4.cloned.1.call-start = ((), (), s32[]{:S(2)}) async-start(), calls=%async_computation.3 | async-start | bytes 5242880 | tf_op jit(solution)/shard_map/all_gather | solution.py:40
  164.6 40.2 %all-to-all-start.2 = ((bf16[2,1024,256]{2,0,1:T(2,128)(2,1)}), bf16[2,1024,256]{2,0,1:T(2,128)(2,1)S(1)}, u32[]{:S(2)}, u32[]{:S(2)}) async-start(bf16[2,1024,256]{2,0,1:T(2,128)(2,1)} %copy.39), calls=%async_computation.2 | async-start | bytes 2097152 | tf_op jit(solution)/shard_map/all_to_all | solution.py:65
  177.2 6.5 %copy-start.2 = (bf16[2,1024,1024]{2,1,0:T(8,128)(2,1)S(1)}, bf16[2,1024,1024]{2,1,0:T(8,128)(2,1)}, u32[]{:S(2)}) copy-start(bf16[2,1024,1024]{2,1,0:T(8,128)(2,1)} %all-gather.4.cloned.1.call-done) | copy-start | bytes 12582916
  177.3 6.5 %copy-start.3 = (f32[1,2,1024,256]{3,2,1,0:T(8,128)S(1)}, f32[1,2,1024,256]{3,2,1,0:T(8,128)}, u32[]{:S(2)}) copy-start(f32[1,2,1024,256]{3,2,1,0:T(8,128)} %param.8) | copy-start | bytes 6291460
Sparse Core Ops, SparseCore 0:
  9.8 70.3 all-gather.5
  102.3 50.3 all-gather.3
where the time goes:
time: 214 us
  waiting for transfers between devices  105 us (49%)
  blocking collectives  42.5 us (20%)
  matrix products  19 us (9%)
  starting transfers between devices  17.1 us (8%)
  between operations  14.2 us (7%)
  local copies, waits for them, and re-layouts  12.5 us (6%)
  other arithmetic  3.46 us (2%)
    all_gather x1, waiting for transfers between devices, on_device(): gradient = lax.all_gather(columns, 'rep', axis=2, tiled=True)  50.5 us
    all_to_all x1, blocking collectives, on_device(): lax.all_to_all(picked.reshape(picked.shape[0], -1, picked.shape[3]), 'fsd...  42.5 us
    all_to_all x1, waiting for transfers between devices, summed_on_arrival(): parts = lax.all_to_all(in_blocks(x, dim, size), axis, 0, 0, tiled=True)  35.2 us
    all_to_all x1, waiting for transfers between devices, on_device(): lax.all_to_all(result_cols, 'fsdp', split_axis=1, concat_axis=0, tiled=True)  18.4 us
    all_to_all x1, starting transfers between devices, on_device(): lax.all_to_all(result_cols, 'fsdp', split_axis=1, concat_axis=0, tiled=True)  12.1 us
    dot_general x1, matrix products, on_device(): jnp.einsum('sik,skj->sij', applied, right_root[0], preferred_element_type...  9.85 us
    dot_general x1, matrix products, on_device(): jnp.einsum('ski,skj->sij', gradient, cols_share, preferred_element_type=j...  6.45 us
    all_to_all x1, starting transfers between devices, summed_on_arrival(): parts = lax.all_to_all(in_blocks(x, dim, size), axis, 0, 0, tiled=True)  4.96 us
  transfers between devices with their start and end apart: 4, of which 3 were waited for; matrix products, arithmetic and copies ran while one was open for 10% of the time, Pallas kernels for 0%

commit v1 on v0

v1 whole, which is shorter than its diff:
```python
import jax
import jax.numpy as jnp
from jax import lax
from jax.experimental import pallas as pl
from jax.experimental.pallas import tpu as pltpu
from jax.sharding import PartitionSpec as P

decay_rate = 0.99

NZ = 8
NY = 8
NX = 4
BLOCKS = 64
HALF = BLOCKS // 2
ROWS = 16
LANES = 128
BS = 1024
SHARE = 256
Z_STEPS = (4, 3, 5, 2, 6, 1, 7)
Y_STEPS = (4, 5, 2, 3, 6, 7, 1)
CHUNK_STEPS = Z_STEPS + (0,)
CHUNKS = 2 * NZ
EARLY = 4
AHEAD = 3


def lanes(index, width):
    return pl.ds(pl.multiple_of(index * width, width), width)


def wait_for(ref, sem):
    pltpu.make_async_copy(ref, ref, sem).wait()


def send(src, dst, send_sem, recv_sem, device):
    pltpu.make_async_remote_copy(
        src_ref=src,
        dst_ref=dst,
        send_sem=send_sem,
        recv_sem=recv_sem,
        device_id=device,
        device_id_type=pl.DeviceIdType.MESH,
    ).start()


def f32(x):
    return x.astype(jnp.float32)


def kernel(
    table, positions, grad, left, right,
    left_out, right_out, update_out,
    gv, relay_p, relay_m, near_p, near_m, far_p, far_m, shares,
    picked, landed, G, L, R, T, U, back, home, left_term, right_term,
    local_sem, rs_s, rs_r, z_s, z_r, y_s, y_r, g_s, g_r, l_s, l_r, bz_s, bz_r, by_s, by_r,
):
    f = lax.axis_index("fsdp")
    x = lax.axis_index("rep")
    z = lax.div(f, NY)
    yc = lax.rem(f, NY)
    nxt = lax.rem(x + 1, NX)
    opp = lax.rem(x + 2, NX)
    prv = lax.rem(x + 3, NX)
    to_nxt = (f, nxt)
    to_prv = (f, prv)

    def z_peer(step):
        return lax.rem(z + step, NZ)

    def y_peer(step):
        return lax.rem(yc + step, NY)

    loads = []
    for k in range(2 * NX):
        loads.append(
            pltpu.make_async_copy(
                grad.at[:, :, pl.ds(k * LANES, LANES)], gv.at[k], local_sem.at[k]
            )
        )
    left_loads = []
    for s in range(2):
        left_loads.append(
            pltpu.make_async_copy(
                left.at[s], L.at[s, :, :, lanes(x, SHARE)], local_sem.at[8 + s]
            )
        )
    right_load = pltpu.make_async_copy(right, R, local_sem.at[10])
    for copy in loads + left_loads + [right_load]:
        copy.start()

    barrier = pltpu.get_barrier_semaphore()
    peers = [to_nxt, to_prv]
    peers += [(z_peer(d) * NY + yc, x) for d in range(1, NZ)]
    peers += [(z * NY + y_peer(d), x) for d in range(1, NY)]
    for peer in peers:
        pl.semaphore_signal(barrier, inc=1, device_id=peer, device_id_type=pl.DeviceIdType.MESH)
    pl.semaphore_wait(barrier, len(peers))

    for copy in loads:
        copy.wait()

    def rs_first(h):
        send(gv.at[opp * 2 + h, pl.ds(0, HALF)], relay_p.at[h], rs_s.at[h, 0], rs_r.at[h, 0], to_nxt)
        send(gv.at[opp * 2 + h, pl.ds(HALF, HALF)], relay_m.at[h], rs_s.at[h, 1], rs_r.at[h, 1], to_prv)
        send(gv.at[nxt * 2 + h, pl.ds(HALF, HALF)], near_p.at[h], rs_s.at[h, 2], rs_r.at[h, 2], to_nxt)
        send(gv.at[prv * 2 + h, pl.ds(0, HALF)], near_m.at[h], rs_s.at[h, 3], rs_r.at[h, 3], to_prv)

    def rs_second(h):
        wait_for(relay_p.at[h], rs_r.at[h, 0])
        relay_p[h] = (f32(relay_p[h]) + f32(gv[nxt * 2 + h, pl.ds(0, HALF)])).astype(jnp.bfloat16)
        send(relay_p.at[h], far_p.at[h], rs_s.at[h, 4], rs_r.at[h, 4], to_nxt)
        wait_for(relay_m.at[h], rs_r.at[h, 1])
        relay_m[h] = (f32(relay_m[h]) + f32(gv[prv * 2 + h, pl.ds(HALF, HALF)])).astype(jnp.bfloat16)
        send(relay_m.at[h], far_m.at[h], rs_s.at[h, 5], rs_r.at[h, 5], to_prv)

    def rs_final(h):
        wait_for(near_p.at[h], rs_r.at[h, 2])
        wait_for(near_m.at[h], rs_r.at[h, 3])
        wait_for(far_p.at[h], rs_r.at[h, 4])
        wait_for(far_m.at[h], rs_r.at[h, 5])
        own = x * 2 + h
        low = f32(gv[own, pl.ds(0, HALF)]) + f32(near_m[h]) + f32(far_p[h])
        shares[h, pl.ds(0, HALF)] = low.astype(jnp.bfloat16)
        high = f32(gv[own, pl.ds(HALF, HALF)]) + f32(near_p[h]) + f32(far_m[h])
        shares[h, pl.ds(HALF, HALF)] = high.astype(jnp.bfloat16)

        def pick(owner, carry):
            for s in range(2):
                block = table[owner, s]
                value = shares[h, jnp.maximum(block, 0)]
                picked[h, s, owner] = jnp.where(block >= 0, value, jnp.zeros_like(value))
            return carry

        lax.fori_loop(0, NZ * NY, pick, 0, unroll=8)

    def z_send(h, s):
        for d in Z_STEPS:
            zp = z_peer(d)
            send(
                picked.at[h, s, pl.ds(zp * NY, NY)], landed.at[h, s, z],
                z_s.at[h, s], z_r.at[h, s], (zp * NY + yc, x),
            )
        landed[h, s, z] = picked[h, s, pl.ds(z * NY, NY)]

    def y_send(h, s):
        wait_for(landed.at[h, s, pl.ds(0, NZ - 1)], z_r.at[h, s])
        where = lanes(x * 2 + h, LANES)
        for d in Y_STEPS:
            yp = y_peer(d)
            send(
                landed.at[h, s, :, yp], G.at[s, :, yc, :, where],
                y_s.at[h, s], y_r.at[h, s], (z * NY + yp, x),
            )
        G[s, :, yc, :, where] = landed[h, s, :, yc]

    def g_send(h, s):
        where = lanes(x * 2 + h, LANES)
        wait_for(G.at[s, :, pl.ds(0, NY - 1), :, where], y_r.at[h, s])
        mine = G.at[s, :, :, :, where]
        send(mine, mine, g_s.at[h, s, 0], g_r.at[h, s, 0], to_nxt)
        send(mine, mine, g_s.at[h, s, 1], g_r.at[h, s, 1], to_prv)

    def g_relay(h, s):
        from_prv = lanes(prv * 2 + h, LANES)
        wait_for(G.at[s, :, :, :, from_prv], g_r.at[h, s, 0])
        part = G.at[s, pl.ds(0, NZ // 2), :, :, from_prv]
        send(part, part, g_s.at[h, s, 2], g_r.at[h, s, 2], to_nxt)
        from_nxt = lanes(nxt * 2 + h, LANES)
        wait_for(G.at[s, :, :, :, from_nxt], g_r.at[h, s, 1])
        part = G.at[s, pl.ds(NZ // 2, NZ // 2), :, :, from_nxt]
        send(part, part, g_s.at[h, s, 3], g_r.at[h, s, 3], to_prv)

    def g_done(h, s):
        where = lanes(opp * 2 + h, LANES)
        wait_for(G.at[s, pl.ds(0, NZ // 2), :, :, where], g_r.at[h, s, 2])
        wait_for(G.at[s, pl.ds(NZ // 2, NZ // 2), :, :, where], g_r.at[h, s, 3])

    def chunk(c):
        return c // NZ, z_peer(CHUNK_STEPS[c % NZ])

    def l_send(c):
        s, zc = chunk(c)
        mine = L.at[s, zc, :, lanes(x, SHARE)]
        send(mine, mine, l_s.at[c, 0], l_r.at[c, 0], to_nxt)
        send(mine, mine, l_s.at[c, 1], l_r.at[c, 1], to_prv)

    def l_relay(c):
        s, zc = chunk(c)
        wait_for(L.at[s, zc, :, lanes(prv, SHARE)], l_r.at[c, 0])
        part = L.at[s, zc, pl.ds(0, LANES // 2), lanes(prv, SHARE)]
        send(part, part, l_s.at[c, 2], l_r.at[c, 2], to_nxt)
        wait_for(L.at[s, zc, :, lanes(nxt, SHARE)], l_r.at[c, 1])
        part = L.at[s, zc, pl.ds(LANES // 2, LANES // 2), lanes(nxt, SHARE)]
        send(part, part, l_s.at[c, 3], l_r.at[c, 3], to_prv)

    def right_product(s):
        @pl.loop(0, NZ // 2)
        def _(i):
            rows = G[s, pl.ds(i * 2, 2)].reshape(SHARE, BS)
            result = jnp.dot(rows, R[s], preferred_element_type=jnp.float32)
            T[s, pl.ds(pl.multiple_of(i * SHARE, SHARE), SHARE), :] = result.astype(jnp.bfloat16)

    def left_statistic(s):
        mine = G[s, pl.ds(x * 2, 2)].reshape(SHARE, BS)

        @pl.loop(0, NZ // 2)
        def _(i):
            rows = G[s, pl.ds(i * 2, 2)].reshape(SHARE, BS)
            result = lax.dot_general(
                rows, mine, (((1,), (1,)), ((), ())), preferred_element_type=jnp.float32
            )
            left_term[s, pl.ds(pl.multiple_of(i * SHARE, SHARE), SHARE), :] = result.astype(jnp.bfloat16)

        pltpu.make_async_copy(left_term.at[s], left_out.at[s], local_sem.at[11 + s]).start()

    def right_statistic(s):
        @pl.loop(0, NX)
        def _(i):
            columns = G[s, :, :, :, lanes(i, SHARE)].reshape(BS, SHARE)
            mine = G[s, :, :, :, lanes(x, SHARE)].reshape(BS, SHARE)
            result = lax.dot_general(
                columns, mine, (((0,), (0,)), ((), ())), preferred_element_type=jnp.float32
            )
            right_term[s, pl.ds(pl.multiple_of(i * SHARE, SHARE), SHARE), :] = result.astype(jnp.bfloat16)

        pltpu.make_async_copy(right_term.at[s], right_out.at[s], local_sem.at[13 + s]).start()

    def update_chunk(c):
        s, zc = chunk(c)
        wait_for(L.at[s, zc, pl.ds(0, LANES // 2), lanes(opp, SHARE)], l_r.at[c, 2])
        wait_for(L.at[s, zc, pl.ds(LANES // 2, LANES // 2), lanes(opp, SHARE)], l_r.at[c, 3])
        result = jnp.dot(L[s, zc], T[s], preferred_element_type=jnp.float32)
        U[s, zc] = result.astype(jnp.bfloat16).reshape(NY, ROWS, SHARE)
        if CHUNK_STEPS[c % NZ] == 0:
            back[s, z] = U[s, z]
        else:
            send(U.at[s, zc], back.at[s, z], bz_s.at[s], bz_r.at[s], (zc * NY + yc, x))

    def back_send(s):
        wait_for(back.at[s, pl.ds(0, NZ - 1)], bz_r.at[s])
        place = pl.ds(s * NZ * NY + yc * NZ, NZ)
        for d in Y_STEPS:
            yp = y_peer(d)
            send(back.at[s, :, yp], home.at[place], by_s.at[s], by_r.at[s], (z * NY + yp, x))
        home[place] = back[s, :, yc]

    rs_first(0)
    rs_second(0)
    rs_first(1)
    rs_final(0)
    z_send(0, 0)
    z_send(0, 1)
    rs_second(1)
    for copy in left_loads:
        copy.wait()
    for c in range(EARLY):
        l_send(c)
    rs_final(1)
    z_send(1, 0)
    z_send(1, 1)
    y_send(0, 0)
    l_relay(0)
    l_relay(1)
    y_send(0, 1)
    g_send(0, 0)
    l_relay(2)
    l_relay(3)
    y_send(1, 0)
    g_send(0, 1)
    g_relay(0, 0)
    y_send(1, 1)
    g_send(1, 0)
    g_relay(0, 1)
    g_send(1, 1)
    g_relay(1, 0)
    for c in range(EARLY, EARLY + AHEAD):
        l_send(c)
    right_load.wait()
    g_done(0, 0)
    g_done(1, 0)
    right_product(0)
    g_relay(1, 1)
    for c in range(EARLY, CHUNKS):
        if c + AHEAD < CHUNKS:
            l_send(c + AHEAD)
        l_relay(c)
        if c == EARLY:
            for early in range(EARLY - 1):
                update_chunk(early)
        if c == EARLY + 1:
            g_done(0, 1)
            g_done(1, 1)
            right_product(1)
        if c == EARLY + 2:
            left_statistic(0)
        if c == EARLY + 3:
            right_statistic(0)
        if c == EARLY + 5:
            left_statistic(1)
        if c == EARLY + 6:
            right_statistic(1)
        update_chunk(c - 1)
        if c == NZ + 2:
            back_send(0)
    update_chunk(CHUNKS - 1)
    back_send(1)
    for s in range(2):
        wait_for(home.at[pl.ds(s * NZ * NY, (NY - 1) * NZ)], by_r.at[s])

    def place_block(b, carry):
        update_out[b] = home[positions[b]]
        return carry

    lax.fori_loop(0, BLOCKS, place_block, 0, unroll=8)

    for h in range(2):
        for k, ref in enumerate((relay_p, relay_m, near_p, near_m, far_p, far_m)):
            wait_for(ref.at[h], rs_s.at[h, k])
        for s in range(2):
            where = lanes(x * 2 + h, LANES)
            wait_for(picked.at[h, s, pl.ds(0, (NZ - 1) * NY)], z_s.at[h, s])
            wait_for(landed.at[h, s, :, pl.ds(0, NY - 1)], y_s.at[h, s])
            for k in range(2):
                wait_for(G.at[s, :, :, :, where], g_s.at[h, s, k])
                wait_for(G.at[s, pl.ds(0, NZ // 2), :, :, where], g_s.at[h, s, 2 + k])
    for c in range(CHUNKS):
        s, zc = chunk(c)
        for k in range(2):
            wait_for(L.at[s, zc, :, lanes(x, SHARE)], l_s.at[c, k])
            wait_for(L.at[s, zc, pl.ds(0, LANES // 2), lanes(x, SHARE)], l_s.at[c, 2 + k])
    for s in range(2):
        wait_for(U.at[s, pl.ds(0, NZ - 1)], bz_s.at[s])
        wait_for(back.at[s, :, pl.ds(0, NY - 1)], by_s.at[s])
        pltpu.make_async_copy(left_term.at[s], left_out.at[s], local_sem.at[11 + s]).wait()
        pltpu.make_async_copy(right_term.at[s], right_out.at[s], local_sem.at[13 + s]).wait()


def exchange(table, positions, grad, left, right):
    bf16 = jnp.bfloat16
    any_spec = pl.BlockSpec(memory_space=pl.ANY)
    smem_spec = pl.BlockSpec(memory_space=pltpu.SMEM)
    dma = pltpu.SemaphoreType.DMA
    half = (2, HALF, ROWS, LANES)
    return pl.pallas_call(
        kernel,
        name="shampoo_exchange",
        out_shape=(
            jax.ShapeDtypeStruct((2, BS, SHARE), bf16),
            jax.ShapeDtypeStruct((2, BS, SHARE), bf16),
            jax.ShapeDtypeStruct((BLOCKS, ROWS, SHARE), bf16),
        ),
        in_specs=[smem_spec, smem_spec, any_spec, any_spec, any_spec],
        out_specs=(any_spec, any_spec, pl.BlockSpec(memory_space=pltpu.VMEM)),
        scratch_shapes=[
            pltpu.VMEM((2 * NX, BLOCKS, ROWS, LANES), bf16),
            pltpu.VMEM(half, bf16),
            pltpu.VMEM(half, bf16),
            pltpu.VMEM(half, bf16),
            pltpu.VMEM(half, bf16),
            pltpu.VMEM(half, bf16),
            pltpu.VMEM(half, bf16),
            pltpu.VMEM((2, BLOCKS, ROWS, LANES), bf16),
            pltpu.VMEM((2, 2, NZ * NY, ROWS, LANES), bf16),
            pltpu.VMEM((2, 2, NZ, NY, ROWS, LANES), bf16),
            pltpu.VMEM((2, NZ, NY, ROWS, BS), bf16),
            pltpu.VMEM((2, NZ, LANES, BS), bf16),
            pltpu.VMEM((2, BS, SHARE), bf16),
            pltpu.VMEM((2, BS, SHARE), bf16),
            pltpu.VMEM((2, NZ, NY, ROWS, SHARE), bf16),
            pltpu.VMEM((2, NZ, NY, ROWS, SHARE), bf16),
            pltpu.VMEM((2 * NZ * NY, ROWS, SHARE), bf16),
            pltpu.VMEM((2, BS, SHARE), bf16),
            pltpu.VMEM((2, BS, SHARE), bf16),
            dma((15,)),
            dma((2, 6)),
            dma((2, 6)),
            dma((2, 2)),
            dma((2, 2)),
            dma((2, 2)),
            dma((2, 2)),
            dma((2, 2, 4)),
            dma((2, 2, 4)),
            dma((CHUNKS, 4)),
            dma((CHUNKS, 4)),
            dma((2,)),
            dma((2,)),
            dma((2,)),
            dma((2,)),
        ],
        compiler_params=pltpu.CompilerParams(
            collective_id=0, has_side_effects=True, vmem_limit_bytes=56 * 1024 * 1024
        ),
        cost_estimate=pl.CostEstimate(
            flops=16 * BS * BS * SHARE, bytes_accessed=16 * BS * BS, transcendentals=0
        ),
    )(table, positions, grad, left, right)


def on_device(partial_grad, owner_table, left_stat, right_stat, left_root, right_root):
    filled = lax.dynamic_index_in_dim(owner_table, lax.axis_index("fsdp"), 0, keepdims=False) >= 0
    flat = owner_table.reshape(NZ, NY, 2).transpose(2, 1, 0).reshape(-1)
    slot_ids = jnp.arange(2 * NZ * NY, dtype=jnp.int32)
    block_ids = jnp.arange(BLOCKS, dtype=jnp.int32)
    positions = jnp.sum(jnp.where(flat[None, :] == block_ids[:, None], slot_ids[None, :], 0), axis=1)
    left_term, right_term, update = exchange(
        owner_table,
        positions,
        partial_grad[0],
        left_root[0].reshape(2, NZ, LANES, SHARE),
        right_root[0],
    )
    keeper = filled[:, None, None]

    def next_of(stat, term):
        moved = decay_rate * stat + (1.0 - decay_rate) * term.astype(jnp.float32)
        return jnp.where(keeper, moved, stat)

    return (
        next_of(left_stat[0], left_term)[None],
        next_of(right_stat[0], right_term)[None],
        update,
    )


def solution(mesh):
    return jax.shard_map(
        on_device,
        mesh=mesh,
        in_specs=(
            P("rep", None, "fsdp", None),
            P(),
            P("fsdp", None, None, "rep"),
            P("fsdp", None, None, "rep"),
            P("fsdp", None, None, "rep"),
            P("fsdp", None, None, "rep"),
        ),
        out_specs=(
            P("fsdp", None, None, "rep"),
            P("fsdp", None, None, "rep"),
            P(None, "fsdp", "rep"),
        ),
        check_vma=False,
    )
```

time: 214 us -> 128 us (0.60)
  Pallas kernels: 0 us -> 118 us
  waiting for transfers between devices: 105 us -> 0 us
  blocking collectives: 42.5 us -> 0 us
  matrix products: 19 us -> 0 us
  starting transfers between devices: 17.1 us -> 0 us
  between operations: 14.2 us -> 0.67 us
  local copies, waits for them, and re-layouts: 12.5 us -> 3.11 us
  other arithmetic: 3.46 us -> 5.84 us
    pallas_call x0 -> x1, Pallas kernels: none -> 118 us  [exchange(): pl.pallas_call(kernel, name='shampoo_exchange', out_shape=(jax.ShapeDtype...]
    all_to_all x2 -> x0, waiting for transfers between devices: 53.6 us -> none  [the longest x1 35.2 us: summed_on_arrival(): parts = lax.all_to_all(in_blocks(x, dim, size), axis, 0, 0, tiled=True)]
    all_gather x2 -> x0, waiting for transfers between devices: 50.5 us -> none  [the longest x1 50.5 us: on_device(): gradient = lax.all_gather(columns, 'rep', axis=2, tiled=True)]
    all_to_all x1 -> x0, blocking collectives: 42.5 us -> none  [on_device(): lax.all_to_all(picked.reshape(picked.shape[0], -1, picked.shape[3]), 'fsd...]
    dot_general x3 -> x0, matrix products: 19 us -> none  [the longest x1 9.85 us: on_device(): jnp.einsum('sik,skj->sij', applied, right_root[0], preferred_element_type...]
    all_to_all x2 -> x0, starting transfers between devices: 17 us -> none  [the longest x1 12.1 us: on_device(): lax.all_to_all(result_cols, 'fsdp', split_axis=1, concat_axis=0, tiled=True)]
    broadcast_in_dim x0 -> x1, other arithmetic: none -> 4.34 us  [on_device(): next_of(right_stat[0], right_term)[None]]
    reshape x1, local copies, waits for them, and re-layouts: 3.33 us -> 0.76 us  [on_device(): flat = owner_table.reshape(NZ, NY, 2).transpose(2, 1, 0).reshape(-1)]
  transfers between devices with their start and end apart: 4 -> 0, of which waited for: 3 -> 0; matrix products, arithmetic and copies ran while one was open for 10% -> 0% of each run, Pallas kernels for 0% -> 0%
where the time goes in v1:
time: 128 us
  Pallas kernels  118 us (92%)
  other arithmetic  5.84 us (5%)
  local copies, waits for them, and re-layouts  3.11 us (2%)
    pallas_call x1, Pallas kernels, exchange(): pl.pallas_call(kernel, name='shampoo_exchange', out_shape=(jax.ShapeDtype...  118 us
    broadcast_in_dim x1, other arithmetic, on_device(): next_of(right_stat[0], right_term)[None]  4.34 us

profile of v1, /device:TPU:1, one launch (start us, length us, event | category | flops | bytes accessed | tf_op | source)
XLA Modules:
  0.0 127.9 jit_solution(13505566128563108103)
XLA Ops:
  0.6 0.9 compare_reduce_fusion
  1.5 0.8 reshape.17
  2.3 0.1 copy.11
  2.3 0.1 eq.15
  2.4 0.6 select_reduce_fusion.positions
  3.1 1.4 %copy.12.table = s32[64,2]{1,0:T(8,128)} copy(s32[64,2]{0,1:T(2,128)} %param.7) | data formatting | bytes 1024 | tf_op args[1]
  4.4 0.0 copy-start
  4.4 0.0 copy-start.1
  4.4 118.3 %shampoo_exchange.1 = (bf16[2,1024,256]{2,1,0:T(8,128)(2,1)}, bf16[2,1024,256]{2,1,0:T(8,128)(2,1)}, bf16[64,16,256]{2,1,0:T(8,128)(2,1)}) custom-call(s32[64,2]{1,0:T(8,128)} %copy.12.table, s32[64]{0:T(128)} %select_reduce_fusion.positions, bf16[64,16,1024]{2,1,0:T(8,128)(2,1)} %bitcast.29, bf16[2,8,128,256]{3,2,1,0:T(8,128)(2,1)} %bitcast.30, ...), custom_call_target="tpu_custom_call" | custom-call | flops 4294967296 | bytes 16777216 | tf_op jit(solution)/shard_map/shampoo_exchange/pallas_call | solution.py:344
  122.8 0.0 copy-done
  122.8 0.0 copy-done.1
  122.8 0.0 copy-start.2
  122.8 4.3 %fusion.1 = (f32[1,2,1024,256]{3,2,1,0:T(8,128)}, f32[1,2,1024,256]{3,2,1,0:T(8,128)}) fusion(f32[1,2,1024,256]{3,2,1,0:T(8,128)S(1)} %copy-done, bf16[2,1024,256]{2,1,0:T(8,128)(2,1)} %get-tuple-element.7, pred[2]{0:T(512)(128)(4,1)S(1)} %compare_reduce_fusion, bf16[2,1024,256]{2,1,0:T(8,128)(2,1)} %get-tuple-element.6, f32[1,2,1024,256]{3,2,1,0:T(8,128)S(1)} %copy-done.1), kind=kLoop, calls=%fused_computation.3 | loop fusion | flops 5242880 | bytes 10485762 | tf_op jit(solution)/shard_map/broadcast_in_dim | solution.py:420
  127.1 0.0 copy-done.2
  127.1 0.8 copy.14
Async XLA Ops:
  4.4 118.3 %copy-start = (f32[1,2,1024,256]{3,2,1,0:T(8,128)S(1)}, f32[1,2,1024,256]{3,2,1,0:T(8,128)}, u32[]{:S(2)}) copy-start(f32[1,2,1024,256]{3,2,1,0:T(8,128)} %param.9) | copy-start | bytes 6291460
  4.4 118.3 %copy-start.1 = (f32[1,2,1024,256]{3,2,1,0:T(8,128)S(1)}, f32[1,2,1024,256]{3,2,1,0:T(8,128)}, u32[]{:S(2)}) copy-start(f32[1,2,1024,256]{3,2,1,0:T(8,128)} %param.8) | copy-start | bytes 6291460
  122.8 4.3 %copy-start.2 = (bf16[64,16,256]{2,1,0:T(8,128)(2,1)S(1)}, bf16[64,16,256]{2,1,0:T(8,128)(2,1)}, u32[]{:S(2)}) copy-start(bf16[64,16,256]{2,1,0:T(8,128)(2,1)} %get-tuple-element.16) | copy-start | bytes 1572868

commit v2 on v1

--- a/solution.py
+++ b/solution.py
@@ -18,10 +18,11 @@
 SHARE = 256
 Z_STEPS = (4, 3, 5, 2, 6, 1, 7)
 Y_STEPS = (4, 5, 2, 3, 6, 7, 1)
-CHUNK_STEPS = Z_STEPS + (0,)
-CHUNKS = 2 * NZ
-EARLY = 4
-AHEAD = 3
+CHUNK_ORDER = (
+    (0, 4), (0, 3), (0, 5), (0, 2), (0, 6), (0, 1), (0, 7), (1, 4),
+    (1, 3), (1, 5), (1, 2), (1, 6), (1, 1), (1, 7), (0, 0), (1, 0),
+)
+CHUNKS = len(CHUNK_ORDER)
 
 
 def lanes(index, width):
@@ -48,9 +49,9 @@
 
 
 def kernel(
-    table, positions, grad, left, right,
-    left_out, right_out, update_out,
-    gv, relay_p, relay_m, near_p, near_m, far_p, far_m, shares,
+    table_hbm, grad, left, right,
+    left_out, right_out, update_out, keep_out,
+    table, table_v, positions, positions_v, gv, relay_p, relay_m, near_p, near_m, far_p, far_m, shares,
     picked, landed, G, L, R, T, U, back, home, left_term, right_term,
     local_sem, rs_s, rs_r, z_s, z_r, y_s, y_r, g_s, g_r, l_s, l_r, bz_s, bz_r, by_s, by_r,
 ):
@@ -70,6 +71,12 @@
     def y_peer(step):
         return lax.rem(yc + step, NY)
 
+    barrier = pltpu.get_barrier_semaphore()
+    peers = [(z_peer(d) * NY + yc, x) for d in Z_STEPS]
+    peers += [(z * NY + y_peer(d), x) for d in Y_STEPS]
+    peers += [to_nxt, to_prv]
+    for peer in peers:
+        pl.semaphore_signal(barrier, inc=1, device_id=peer, device_id_type=pl.DeviceIdType.MESH)
     loads = []
     for k in range(2 * NX):
         loads.append(
@@ -85,15 +92,13 @@
             )
         )
     right_load = pltpu.make_async_copy(right, R, local_sem.at[10])
-    for copy in loads + left_loads + [right_load]:
+    table_loads = [
+        pltpu.make_async_copy(table_hbm, table, local_sem.at[15]),
+        pltpu.make_async_copy(table_hbm, table_v, local_sem.at[16]),
+    ]
+    for copy in loads + table_loads + left_loads + [right_load]:
         copy.start()
 
-    barrier = pltpu.get_barrier_semaphore()
-    peers = [to_nxt, to_prv]
-    peers += [(z_peer(d) * NY + yc, x) for d in range(1, NZ)]
-    peers += [(z * NY + y_peer(d), x) for d in range(1, NY)]
-    for peer in peers:
-        pl.semaphore_signal(barrier, inc=1, device_id=peer, device_id_type=pl.DeviceIdType.MESH)
     pl.semaphore_wait(barrier, len(peers))
 
     for copy in loads:
@@ -126,7 +131,7 @@
 
         def pick(owner, carry):
             for s in range(2):
-                block = table[owner, s]
+                block = table[s, owner]
                 value = shares[h, jnp.maximum(block, 0)]
                 picked[h, s, owner] = jnp.where(block >= 0, value, jnp.zeros_like(value))
             return carry
@@ -176,22 +181,23 @@
         wait_for(G.at[s, pl.ds(NZ // 2, NZ // 2), :, :, where], g_r.at[h, s, 3])
 
     def chunk(c):
-        return c // NZ, z_peer(CHUNK_STEPS[c % NZ])
+        s, step = CHUNK_ORDER[c]
+        return s, z_peer(step)
 
     def l_send(c):
         s, zc = chunk(c)
         mine = L.at[s, zc, :, lanes(x, SHARE)]
-        send(mine, mine, l_s.at[c, 0], l_r.at[c, 0], to_nxt)
-        send(mine, mine, l_s.at[c, 1], l_r.at[c, 1], to_prv)
+        send(mine, mine, l_s.at[0], l_r.at[c, 0], to_nxt)
+        send(mine, mine, l_s.at[1], l_r.at[c, 1], to_prv)
 
     def l_relay(c):
         s, zc = chunk(c)
         wait_for(L.at[s, zc, :, lanes(prv, SHARE)], l_r.at[c, 0])
         part = L.at[s, zc, pl.ds(0, LANES // 2), lanes(prv, SHARE)]
-        send(part, part, l_s.at[c, 2], l_r.at[c, 2], to_nxt)
+        send(part, part, l_s.at[2], l_r.at[c, 2], to_nxt)
         wait_for(L.at[s, zc, :, lanes(nxt, SHARE)], l_r.at[c, 1])
         part = L.at[s, zc, pl.ds(LANES // 2, LANES // 2), lanes(nxt, SHARE)]
-        send(part, part, l_s.at[c, 3], l_r.at[c, 3], to_prv)
+        send(part, part, l_s.at[3], l_r.at[c, 3], to_prv)
 
     def right_product(s):
         @pl.loop(0, NZ // 2)
@@ -231,88 +237,130 @@
         wait_for(L.at[s, zc, pl.ds(LANES // 2, LANES // 2), lanes(opp, SHARE)], l_r.at[c, 3])
         result = jnp.dot(L[s, zc], T[s], preferred_element_type=jnp.float32)
         U[s, zc] = result.astype(jnp.bfloat16).reshape(NY, ROWS, SHARE)
-        if CHUNK_STEPS[c % NZ] == 0:
+        if CHUNK_ORDER[c][1] == 0:
             back[s, z] = U[s, z]
         else:
-            send(U.at[s, zc], back.at[s, z], bz_s.at[s], bz_r.at[s], (zc * NY + yc, x))
-
-    def back_send(s):
-        wait_for(back.at[s, pl.ds(0, NZ - 1)], bz_r.at[s])
-        place = pl.ds(s * NZ * NY + yc * NZ, NZ)
+            send(U.at[s, zc], back.at[s, z], bz_s.at[s], bz_r.at[c], (zc * NY + yc, x))
+
+    def back_send(c):
+        s, step = CHUNK_ORDER[c]
+        source = lax.rem(z + NZ - step, NZ)
+        if step != 0:
+            wait_for(back.at[s, source], bz_r.at[c])
+        place = s * NZ * NY + yc * NZ + source
         for d in Y_STEPS:
             yp = y_peer(d)
-            send(back.at[s, :, yp], home.at[place], by_s.at[s], by_r.at[s], (z * NY + yp, x))
-        home[place] = back[s, :, yc]
+            send(back.at[s, source, yp], home.at[place], by_s.at[s], by_r.at[s], (z * NY + yp, x))
+        home[place] = back[s, source, yc]
+
+    def find_positions():
+        table_loads[1].wait()
+        total = jnp.zeros((1, LANES), jnp.int32)
+        owner = lax.broadcasted_iota(jnp.int32, (NZ * NY, LANES), 0)
+        block = lax.broadcasted_iota(jnp.int32, (NZ * NY, LANES), 1)
+        slot = lax.rem(owner, NY) * NZ + lax.div(owner, NY)
+        for s in range(2):
+            row = table_v[pl.ds(s, 1), :]
+            held = jnp.broadcast_to(row, (LANES, NZ * NY)).T
+            hit = jnp.where(held == block, slot + s * NZ * NY, 0)
+            total += jnp.sum(hit, axis=0, keepdims=True)
+        positions_v[...] = jnp.minimum(total, 2 * NZ * NY - 1)
+        copy = pltpu.make_async_copy(positions_v, positions, local_sem.at[17])
+        copy.start()
+        copy.wait()
+        for s in range(2):
+            factor = jnp.where(table[s, f] >= 0, decay_rate, 1.0).astype(jnp.float32)
+            keep_out[s] = jnp.full((8, LANES), factor, jnp.float32)
 
     rs_first(0)
+    left_loads[0].wait()
+    l_send(0)
     rs_second(0)
     rs_first(1)
+    l_send(1)
+    table_loads[0].wait()
     rs_final(0)
     z_send(0, 0)
-    z_send(0, 1)
     rs_second(1)
-    for copy in left_loads:
-        copy.wait()
-    for c in range(EARLY):
+    for c in range(2, 6):
         l_send(c)
+    find_positions()
     rs_final(1)
     z_send(1, 0)
+    z_send(0, 1)
     z_send(1, 1)
     y_send(0, 0)
     l_relay(0)
     l_relay(1)
-    y_send(0, 1)
-    g_send(0, 0)
+    l_send(6)
     l_relay(2)
     l_relay(3)
+    g_send(0, 0)
+    l_relay(4)
+    l_relay(5)
     y_send(1, 0)
+    l_relay(6)
+    g_send(1, 0)
+    y_send(0, 1)
+    g_relay(0, 0)
     g_send(0, 1)
-    g_relay(0, 0)
     y_send(1, 1)
-    g_send(1, 0)
+    g_relay(1, 0)
+    g_send(1, 1)
+    right_load.wait()
+    left_loads[1].wait()
     g_relay(0, 1)
-    g_send(1, 1)
-    g_relay(1, 0)
-    for c in range(EARLY, EARLY + AHEAD):
-        l_send(c)
-    right_load.wait()
+    l_send(7)
     g_done(0, 0)
     g_done(1, 0)
     right_product(0)
+    for c in range(0, 7):
+        update_chunk(c)
+    left_statistic(0)
     g_relay(1, 1)
-    for c in range(EARLY, CHUNKS):
-        if c + AHEAD < CHUNKS:
-            l_send(c + AHEAD)
-        l_relay(c)
-        if c == EARLY:
-            for early in range(EARLY - 1):
-                update_chunk(early)
-        if c == EARLY + 1:
-            g_done(0, 1)
-            g_done(1, 1)
-            right_product(1)
-        if c == EARLY + 2:
-            left_statistic(0)
-        if c == EARLY + 3:
-            right_statistic(0)
-        if c == EARLY + 5:
-            left_statistic(1)
-        if c == EARLY + 6:
-            right_statistic(1)
-        update_chunk(c - 1)
-        if c == NZ + 2:
-            back_send(0)
-    update_chunk(CHUNKS - 1)
+    l_send(8)
+    l_send(9)
+    l_send(10)
+    right_statistic(0)
+    l_relay(7)
+    l_send(11)
+    g_done(0, 1)
+    g_done(1, 1)
+    right_product(1)
+    l_relay(8)
+    l_send(12)
+    left_statistic(1)
+    l_relay(9)
+    l_send(13)
+    right_statistic(1)
+    l_relay(10)
+    l_send(14)
+    update_chunk(7)
+    l_relay(11)
+    l_send(15)
+    update_chunk(8)
+    back_send(2)
+    back_send(0)
+    l_relay(12)
+    update_chunk(9)
+    back_send(4)
     back_send(1)
-    for s in range(2):
-        wait_for(home.at[pl.ds(s * NZ * NY, (NY - 1) * NZ)], by_r.at[s])
-
-    def place_block(b, carry):
-        update_out[b] = home[positions[b]]
-        return carry
-
-    lax.fori_loop(0, BLOCKS, place_block, 0, unroll=8)
-
+    l_relay(13)
+    update_chunk(10)
+    back_send(5)
+    back_send(3)
+    l_relay(14)
+    update_chunk(11)
+    l_relay(15)
+    update_chunk(12)
+    update_chunk(13)
+    back_send(6)
+    update_chunk(14)
+    back_send(14)
+    update_chunk(15)
+    back_send(15)
+    for c in range(7, 14):
+        back_send(c)
     for h in range(2):
         for k, ref in enumerate((relay_p, relay_m, near_p, near_m, far_p, far_m)):
             wait_for(ref.at[h], rs_s.at[h, k])
@@ -323,22 +371,32 @@
             for k in range(2):
                 wait_for(G.at[s, :, :, :, where], g_s.at[h, s, k])
                 wait_for(G.at[s, pl.ds(0, NZ // 2), :, :, where], g_s.at[h, s, 2 + k])
-    for c in range(CHUNKS):
-        s, zc = chunk(c)
-        for k in range(2):
-            wait_for(L.at[s, zc, :, lanes(x, SHARE)], l_s.at[c, k])
-            wait_for(L.at[s, zc, pl.ds(0, LANES // 2), lanes(x, SHARE)], l_s.at[c, 2 + k])
+    for k in range(2):
+        wait_for(L.at[:, :, :, lanes(x, SHARE)], l_s.at[k])
+        wait_for(L.at[0, :, :, lanes(x, SHARE)], l_s.at[2 + k])
     for s in range(2):
         wait_for(U.at[s, pl.ds(0, NZ - 1)], bz_s.at[s])
-        wait_for(back.at[s, :, pl.ds(0, NY - 1)], by_s.at[s])
         pltpu.make_async_copy(left_term.at[s], left_out.at[s], local_sem.at[11 + s]).wait()
         pltpu.make_async_copy(right_term.at[s], right_out.at[s], local_sem.at[13 + s]).wait()
 
-
-def exchange(table, positions, grad, left, right):
+    for s in range(2):
+        wait_for(home.at[pl.ds(s * NZ * NY, (NY - 1) * NZ)], by_r.at[s])
+
+    def place_block(b, carry):
+        update_out[b] = home[positions[0, b]]
+        return carry
+
+    lax.fori_loop(0, BLOCKS, place_block, 0, unroll=8)
+
+    for s in range(2):
+        wait_for(back.at[s, :, pl.ds(0, NY - 1)], by_s.at[s])
+
+
+def exchange(table, grad, left, right):
     bf16 = jnp.bfloat16
     any_spec = pl.BlockSpec(memory_space=pl.ANY)
-    smem_spec = pl.BlockSpec(memory_space=pltpu.SMEM)
+    hbm_spec = pl.BlockSpec(memory_space=pltpu.HBM)
+    vmem_spec = pl.BlockSpec(memory_space=pltpu.VMEM)
     dma = pltpu.SemaphoreType.DMA
     half = (2, HALF, ROWS, LANES)
     return pl.pallas_call(
@@ -348,10 +406,15 @@
             jax.ShapeDtypeStruct((2, BS, SHARE), bf16),
             jax.ShapeDtypeStruct((2, BS, SHARE), bf16),
             jax.ShapeDtypeStruct((BLOCKS, ROWS, SHARE), bf16),
+            jax.ShapeDtypeStruct((2, 8, LANES), jnp.float32),
         ),
-        in_specs=[smem_spec, smem_spec, any_spec, any_spec, any_spec],
-        out_specs=(any_spec, any_spec, pl.BlockSpec(memory_space=pltpu.VMEM)),
+        in_specs=[hbm_spec, hbm_spec, hbm_spec, hbm_spec],
+        out_specs=(any_spec, any_spec, vmem_spec, vmem_spec),
         scratch_shapes=[
+            pltpu.SMEM((2, NZ * NY), jnp.int32),
+            pltpu.VMEM((2, NZ * NY), jnp.int32),
+            pltpu.SMEM((1, LANES), jnp.int32),
+            pltpu.VMEM((1, LANES), jnp.int32),
             pltpu.VMEM((2 * NX, BLOCKS, ROWS, LANES), bf16),
             pltpu.VMEM(half, bf16),
             pltpu.VMEM(half, bf16),
@@ -371,7 +434,7 @@
             pltpu.VMEM((2 * NZ * NY, ROWS, SHARE), bf16),
             pltpu.VMEM((2, BS, SHARE), bf16),
             pltpu.VMEM((2, BS, SHARE), bf16),
-            dma((15,)),
+            dma((18,)),
             dma((2, 6)),
             dma((2, 6)),
             dma((2, 2)),
@@ -380,46 +443,78 @@
             dma((2, 2)),
             dma((2, 2, 4)),
             dma((2, 2, 4)),
-            dma((CHUNKS, 4)),
+            dma((4,)),
             dma((CHUNKS, 4)),
             dma((2,)),
-            dma((2,)),
+            dma((CHUNKS,)),
             dma((2,)),
             dma((2,)),
         ],
         compiler_params=pltpu.CompilerParams(
-            collective_id=0, has_side_effects=True, vmem_limit_bytes=56 * 1024 * 1024
+            collective_id=0, has_side_effects=True, vmem_limit_bytes=51 * 1024 * 1024
         ),
         cost_estimate=pl.CostEstimate(
             flops=16 * BS * BS * SHARE, bytes_accessed=16 * BS * BS, transcendentals=0
         ),
-    )(table, positions, grad, left, right)
+    )(table, grad, left, right)
+
+
+def finish_kernel(
+    left_stat, right_stat, left_term, right_term, update, keep,
+    left_next, right_next, update_out,
+    left_new, right_new, sem,
+):
+    copies = [pltpu.make_async_copy(update, update_out, sem.at[0])]
+    copies[0].start()
+    for s in range(2):
+        factor = keep[s][:1, :1]
+        for side, (stat, term, new, out) in enumerate((
+            (left_stat, left_term, left_new, left_next),
+            (right_stat, right_term, right_new, right_next),
+        )):
+            for part in range(2):
+                rows = pl.ds(part * (BS // 2), BS // 2)
+                new[s, rows] = factor * stat[s, rows] + (1.0 - decay_rate) * f32(term[s, rows])
+                copy = pltpu.make_async_copy(
+                    new.at[s, rows], out.at[s, rows], sem.at[1 + s * 4 + side * 2 + part]
+                )
+                copy.start()
+                copies.append(copy)
+    for copy in copies:
+        copy.wait()
+
+
+def finish(left_stat, right_stat, left_term, right_term, update, keep):
+    vmem_spec = pl.BlockSpec(memory_space=pltpu.VMEM)
+    stat_shape = jax.ShapeDtypeStruct((2, BS, SHARE), jnp.float32)
+    return pl.pallas_call(
+        finish_kernel,
+        name="shampoo_finish",
+        out_shape=(stat_shape, stat_shape, jax.ShapeDtypeStruct(update.shape, update.dtype)),
+        in_specs=[vmem_spec] * 6,
+        out_specs=(pl.BlockSpec(memory_space=pl.ANY),) * 3,
+        scratch_shapes=[
+            pltpu.VMEM((2, BS, SHARE), jnp.float32),
+            pltpu.VMEM((2, BS, SHARE), jnp.float32),
+            pltpu.SemaphoreType.DMA((9,)),
+        ],
+        compiler_params=pltpu.CompilerParams(vmem_limit_bytes=24 * 1024 * 1024),
+        cost_estimate=pl.CostEstimate(flops=4 * BS * BS, bytes_accessed=8 * BS * BS, transcendentals=0),
+    )(left_stat, right_stat, left_term, right_term, update, keep)
 
 
 def on_device(partial_grad, owner_table, left_stat, right_stat, left_root, right_root):
-    filled = lax.dynamic_index_in_dim(owner_table, lax.axis_index("fsdp"), 0, keepdims=False) >= 0
-    flat = owner_table.reshape(NZ, NY, 2).transpose(2, 1, 0).reshape(-1)
-    slot_ids = jnp.arange(2 * NZ * NY, dtype=jnp.int32)
-    block_ids = jnp.arange(BLOCKS, dtype=jnp.int32)
-    positions = jnp.sum(jnp.where(flat[None, :] == block_ids[:, None], slot_ids[None, :], 0), axis=1)
-    left_term, right_term, update = exchange(
-        owner_table,
-        positions,
+    left_term, right_term, update, keep = exchange(
+        owner_table.T,
         partial_grad[0],
         left_root[0].reshape(2, NZ, LANES, SHARE),
         right_root[0],
     )
-    keeper = filled[:, None, None]
-
-    def next_of(stat, term):
-        moved = decay_rate * stat + (1.0 - decay_rate) * term.astype(jnp.float32)
-        return jnp.where(keeper, moved, stat)
-
-    return (
-        next_of(left_stat[0], left_term)[None],
-        next_of(right_stat[0], right_term)[None],
-        update,
+
+    left_next, right_next, update = finish(
+        left_stat[0], right_stat[0], left_term, right_term, update, keep
     )
+    return left_next[None], right_next[None], update
 
 
 def solution(mesh):

time: 128 us -> 110 us (0.86)
  Pallas kernels: 118 us -> 109 us
  other arithmetic: 5.84 us -> 0 us
  local copies, waits for them, and re-layouts: 3.11 us -> 0.68 us
    pallas_call x1, Pallas kernels: 118 us -> 107 us  [exchange(): pl.pallas_call(kernel, name='shampoo_exchange', out_shape=(jax.ShapeDtype...]
    broadcast_in_dim x1 -> x0, other arithmetic: 4.34 us -> none  [on_device(): next_of(right_stat[0], right_term)[None]]
    pallas_call x0 -> x1, Pallas kernels: none -> 2.25 us  [finish(): pl.pallas_call(finish_kernel, name='shampoo_finish', out_shape=(stat_shap...]
    unnamed x8 -> x6, local copies, waits for them, and re-layouts: 2.19 us -> 0.68 us
where the time goes in v2:
time: 110 us
  Pallas kernels  109 us (99%)
    pallas_call x1, Pallas kernels, exchange(): pl.pallas_call(kernel, name='shampoo_exchange', out_shape=(jax.ShapeDtype...  107 us
    pallas_call x1, Pallas kernels, finish(): pl.pallas_call(finish_kernel, name='shampoo_finish', out_shape=(stat_shap...  2.25 us

profile of v2, /device:TPU:1, one launch (start us, length us, event | category | flops | bytes accessed | tf_op | source)
XLA Modules:
  0.0 110.4 jit_solution(4287864854913554157)
XLA Ops:
  0.6 0.0 copy-start.2
  0.6 0.7 copy-done.2
  1.3 0.0 copy-start
  1.3 0.0 copy-start.1
  1.3 106.8 %shampoo_exchange.1 = (bf16[2,1024,256]{2,1,0:T(8,128)(2,1)S(1)}, bf16[2,1024,256]{2,1,0:T(8,128)(2,1)S(1)}, bf16[64,16,256]{2,1,0:T(8,128)(2,1)S(1)}, f32[2,8,128]{2,1,0:T(8,128)S(1)}) custom-call(s32[2,64]{1,0:T(2,128)S(1)} %bitcast.10, bf16[64,16,1024]{2,1,0:T(8,128)(2,1)} %bitcast.11, bf16[2,8,128,256]{3,2,1,0:T(8,128)(2,1)} %bitcast.14, ...), custom_call_target="tpu_custom_call" | custom-call | flops 4294967296 | bytes 16777216 | tf_op jit(solution)/shard_map/shampoo_exchange/pallas_call | solution.py:402
  108.1 0.0 copy-done
  108.1 0.0 copy-done.1
  108.1 2.3 %shampoo_finish.1 = (f32[2,1024,256]{2,1,0:T(8,128)}, f32[2,1024,256]{2,1,0:T(8,128)}, bf16[64,16,256]{2,1,0:T(8,128)(2,1)}) custom-call(f32[2,1024,256]{2,1,0:T(8,128)S(1)} %bitcast.8, f32[2,1024,256]{2,1,0:T(8,128)S(1)} %bitcast.9, bf16[2,1024,256]{2,1,0:T(8,128)(2,1)S(1)} %get-tuple-element.10.left_term, ...), custom_call_target="tpu_custom_call" | custom-call | flops 4194304 | bytes 8388608 | tf_op jit(solution)/shard_map/shampoo_finish/pallas_call | solution.py:490
Async XLA Ops:
  0.6 0.7 copy-start.2
  1.3 106.8 %copy-start = (f32[1,2,1024,256]{3,2,1,0:T(8,128)S(1)}, f32[1,2,1024,256]{3,2,1,0:T(8,128)}, u32[]{:S(2)}) copy-start(f32[1,2,1024,256]{3,2,1,0:T(8,128)} %param.8) | copy-start | bytes 6291460
  1.3 106.8 %copy-start.1 = (f32[1,2,1024,256]{3,2,1,0:T(8,128)S(1)}, f32[1,2,1024,256]{3,2,1,0:T(8,128)}, u32[]{:S(2)}) copy-start(f32[1,2,1024,256]{3,2,1,0:T(8,128)} %param.9) | copy-start | bytes 6291460

commit v3 on v2

v3 whole, which is shorter than its diff:
```python
import jax
import jax.numpy as jnp
from jax import lax
from jax.experimental import pallas as pl
from jax.experimental.pallas import tpu as pltpu
from jax.sharding import PartitionSpec as P

decay_rate = 0.99

NZ = 8
NY = 8
NX = 4
BLOCKS = 64
HALF = BLOCKS // 2
ROWS = 16
LANES = 128
BS = 1024
SHARE = 256
Z_STEPS = (4, 3, 5, 2, 6, 1, 7)
Y_STEPS = (4, 5, 2, 3, 6, 7, 1)
CHUNK_ORDER = (
    (0, 4), (0, 3), (0, 5), (0, 2), (0, 6), (1, 4), (1, 3), (0, 1),
    (0, 7), (1, 5), (1, 2), (1, 6), (1, 1), (1, 7), (0, 0), (1, 0),
)
CHUNKS = len(CHUNK_ORDER)
BACKWARD = (9, 10, 11, 12)


def lanes(index, width):
    return pl.ds(pl.multiple_of(index * width, width), width)


def wait_for(ref, sem):
    pltpu.make_async_copy(ref, ref, sem).wait()


def send(src, dst, send_sem, recv_sem, device):
    pltpu.make_async_remote_copy(
        src_ref=src,
        dst_ref=dst,
        send_sem=send_sem,
        recv_sem=recv_sem,
        device_id=device,
        device_id_type=pl.DeviceIdType.MESH,
    ).start()


def f32(x):
    return x.astype(jnp.float32)


def kernel(
    table_hbm, grad, left, right,
    left_out, right_out, home, positions_out, keep_out,
    table, table_v, positions, keep, gv, relay_p, relay_m, near_p, near_m, far_p, far_m, shares, copied,
    picked, landed, G, L, R, T, U, back, left_term, right_term,
    local_sem, home_sem, share_sem, rs_s, rs_r, z_s, z_r, y_s, y_r, g_s, g_r, l_s, l_r, bz_s, bz_r, by_s, by_r,
):
    f = lax.axis_index("fsdp")
    x = lax.axis_index("rep")
    z = lax.div(f, NY)
    yc = lax.rem(f, NY)
    nxt = lax.rem(x + 1, NX)
    opp = lax.rem(x + 2, NX)
    prv = lax.rem(x + 3, NX)
    to_nxt = (f, nxt)
    to_prv = (f, prv)

    def z_peer(step):
        return lax.rem(z + step, NZ)

    def y_peer(step):
        return lax.rem(yc + step, NY)

    barrier = pltpu.get_barrier_semaphore()
    peers = [(z_peer(d) * NY + yc, x) for d in Z_STEPS]
    peers += [(z * NY + y_peer(d), x) for d in Y_STEPS]
    peers += [to_nxt, to_prv]
    for peer in peers:
        pl.semaphore_signal(barrier, inc=1, device_id=peer, device_id_type=pl.DeviceIdType.MESH)
    loads = []
    for k in range(2 * NX):
        loads.append(
            pltpu.make_async_copy(
                grad.at[:, :, pl.ds(k * LANES, LANES)], gv.at[k], local_sem.at[0]
            )
        )
    left_loads = []
    for s in range(2):
        left_loads.append(
            pltpu.make_async_copy(
                left.at[s], L.at[s, :, :, lanes(x, SHARE)], local_sem.at[1 + s]
            )
        )
    right_load = pltpu.make_async_copy(right, R, local_sem.at[3])
    table_loads = [
        pltpu.make_async_copy(table_hbm, table, local_sem.at[5]),
        pltpu.make_async_copy(table_hbm, table_v, local_sem.at[6]),
    ]
    for copy in loads + table_loads + left_loads + [right_load]:
        copy.start()

    pl.semaphore_wait(barrier, len(peers))

    wait_for(gv, local_sem.at[0])

    def rs_send(src, dst, kind, h, peer):
        send(src, dst, rs_s.at[kind], rs_r.at[h, min(kind, 2)], peer)

    def rs_first(h):
        rs_send(gv.at[opp * 2 + h, pl.ds(0, HALF)], relay_p.at[h], 0, h, to_nxt)
        rs_send(gv.at[opp * 2 + h, pl.ds(HALF, HALF)], relay_m.at[h], 1, h, to_prv)
        rs_send(gv.at[nxt * 2 + h, pl.ds(HALF, HALF)], near_p.at[h], 2, h, to_nxt)
        rs_send(gv.at[prv * 2 + h, pl.ds(0, HALF)], near_m.at[h], 3, h, to_prv)

    def rs_second(h):
        wait_for(relay_p.at[h], rs_r.at[h, 0])
        relay_p[h] = (f32(relay_p[h]) + f32(gv[nxt * 2 + h, pl.ds(0, HALF)])).astype(jnp.bfloat16)
        rs_send(relay_p.at[h], far_p.at[h], 4, h, to_nxt)
        wait_for(relay_m.at[h], rs_r.at[h, 1])
        relay_m[h] = (f32(relay_m[h]) + f32(gv[prv * 2 + h, pl.ds(HALF, HALF)])).astype(jnp.bfloat16)
        rs_send(relay_m.at[h], far_m.at[h], 5, h, to_prv)

    def pick_from(kind):
        def pick(owner, carry):
            for s in range(2):
                block = table[s, owner]
                index = jnp.maximum(block, 0)
                value = copied[index] if kind == 2 else shares[kind, index]
                picked[kind, s, owner] = jnp.where(block >= 0, value, jnp.zeros_like(value))
            return carry

        lax.fori_loop(0, NZ * NY, pick, 0, unroll=8)

    def rs_final(h):
        wait_for(gv.at[pl.ds(0, 2)], rs_r.at[h, 2])
        own = x * 2 + h
        low = f32(gv[own, pl.ds(0, HALF)]) + f32(near_m[h]) + f32(far_p[h])
        shares[h, pl.ds(0, HALF)] = low.astype(jnp.bfloat16)
        high = f32(gv[own, pl.ds(HALF, HALF)]) + f32(near_p[h]) + f32(far_m[h])
        shares[h, pl.ds(HALF, HALF)] = high.astype(jnp.bfloat16)
        pick_from(h)

    def share_send():
        send(shares.at[0], copied, share_sem.at[0], share_sem.at[1], to_nxt)

    def share_pick():
        wait_for(copied, share_sem.at[1])
        pick_from(2)

    def place_of(kind):
        return lanes(prv * 2 if kind == 2 else x * 2 + kind, LANES)

    def z_send(kind, s):
        for d in Z_STEPS:
            zp = z_peer(d)
            send(
                picked.at[kind, s, pl.ds(zp * NY, NY)], landed.at[kind, s, z],
                z_s.at[0], z_r.at[kind, s], (zp * NY + yc, x),
            )
        landed[kind, s, z] = picked[kind, s, pl.ds(z * NY, NY)]

    def y_send(kind, s):
        wait_for(landed.at[kind, s, pl.ds(0, NZ - 1)], z_r.at[kind, s])
        where = place_of(kind)
        for d in Y_STEPS:
            yp = y_peer(d)
            send(
                landed.at[kind, s, :, yp], G.at[s, :, yc, :, where],
                y_s.at[0], y_r.at[kind, s], (z * NY + yp, x),
            )
        G[s, :, yc, :, where] = landed[kind, s, :, yc]

    def g_send(kind, s):
        where = place_of(kind)
        wait_for(G.at[s, :, pl.ds(0, NY - 1), :, where], y_r.at[kind, s])
        mine = G.at[s, :, :, :, where]
        if kind != 0:
            send(mine, mine, g_s.at[0], g_r.at[kind - 1, s, 0], to_nxt)
        if kind != 2:
            send(mine, mine, g_s.at[1], g_r.at[1 - kind, s, 1], to_prv)

    def g_relay_p(s):
        where = lanes(prv * 2 + 1, LANES)
        wait_for(G.at[s, :, :, :, where], g_r.at[0, s, 0])
        part = G.at[s, pl.ds(0, NZ // 2), :, :, where]
        send(part, part, g_s.at[2], g_r.at[0, s, 2], to_nxt)

    def g_relay_m(s):
        where = lanes(nxt * 2 + 1, LANES)
        wait_for(G.at[s, :, :, :, where], g_r.at[0, s, 1])
        part = G.at[s, pl.ds(NZ // 2, NZ // 2), :, :, where]
        send(part, part, g_s.at[3], g_r.at[0, s, 2], to_prv)

    def g_done(s):
        wait_for(G.at[s, :, :, :, lanes(nxt * 2, LANES)], g_r.at[1, s, 1])
        wait_for(G.at[s, :, :, :, lanes(opp * 2, LANES)], g_r.at[1, s, 0])
        wait_for(G.at[s, :, :, :, lanes(opp * 2 + 1, LANES)], g_r.at[0, s, 2])

    def chunk(c):
        s, step = CHUNK_ORDER[c]
        return s, z_peer(step)

    def l_send_p(c):
        s, zc = chunk(c)
        mine = L.at[s, zc, :, lanes(x, SHARE)]
        send(mine, mine, l_s.at[0], l_r.at[c, 0], to_nxt)

    def l_send_m(c):
        s, zc = chunk(c)
        mine = L.at[s, zc, :, lanes(x, SHARE)]
        send(mine, mine, l_s.at[1], l_r.at[c, 1], to_prv)

    def l_send(c):
        l_send_p(c)
        l_send_m(c)

    def l_relay_p(c):
        s, zc = chunk(c)
        wait_for(L.at[s, zc, :, lanes(prv, SHARE)], l_r.at[c, 0])
        if c not in BACKWARD:
            part = L.at[s, zc, pl.ds(0, LANES // 2), lanes(prv, SHARE)]
            send(part, part, l_s.at[2], l_r.at[c, 2], to_nxt)

    def l_relay_m(c):
        s, zc = chunk(c)
        wait_for(L.at[s, zc, :, lanes(nxt, SHARE)], l_r.at[c, 1])
        first = 0 if c in BACKWARD else LANES // 2
        part = L.at[s, zc, pl.ds(first, LANES - first), lanes(nxt, SHARE)]
        send(part, part, l_s.at[3], l_r.at[c, 2], to_prv)

    def l_relay(c):
        l_relay_p(c)
        l_relay_m(c)

    def right_product(s):
        @pl.loop(0, NZ // 2)
        def _(i):
            rows = G[s, pl.ds(i * 2, 2)].reshape(SHARE, BS)
            result = jnp.dot(rows, R[s], preferred_element_type=jnp.float32)
            T[s, pl.ds(pl.multiple_of(i * SHARE, SHARE), SHARE), :] = result.astype(jnp.bfloat16)

    def left_statistic(s):
        mine = G[s, pl.ds(x * 2, 2)].reshape(SHARE, BS)

        @pl.loop(0, NZ // 2)
        def _(i):
            rows = G[s, pl.ds(i * 2, 2)].reshape(SHARE, BS)
            result = lax.dot_general(
                rows, mine, (((1,), (1,)), ((), ())), preferred_element_type=jnp.float32
            )
            left_term[s, pl.ds(pl.multiple_of(i * SHARE, SHARE), SHARE), :] = result.astype(jnp.bfloat16)

        pltpu.make_async_copy(left_term.at[s], left_out.at[s], local_sem.at[4]).start()

    def right_statistic(s):
        @pl.loop(0, NX)
        def _(i):
            columns = G[s, :, :, :, lanes(i, SHARE)].reshape(BS, SHARE)
            mine = G[s, :, :, :, lanes(x, SHARE)].reshape(BS, SHARE)
            result = lax.dot_general(
                columns, mine, (((0,), (0,)), ((), ())), preferred_element_type=jnp.float32
            )
            right_term[s, pl.ds(pl.multiple_of(i * SHARE, SHARE), SHARE), :] = result.astype(jnp.bfloat16)

        pltpu.make_async_copy(right_term.at[s], right_out.at[s], local_sem.at[4]).start()

    def update_chunk(c):
        s, zc = chunk(c)
        wait_for(L.at[s, zc, :, lanes(opp, SHARE)], l_r.at[c, 2])
        result = jnp.dot(L[s, zc], T[s], preferred_element_type=jnp.float32)
        U[s, zc] = result.astype(jnp.bfloat16).reshape(NY, ROWS, SHARE)
        if CHUNK_ORDER[c][1] == 0:
            back[s, z] = U[s, z]
        else:
            send(U.at[s, zc], back.at[s, z], bz_s.at[0], bz_r.at[c], (zc * NY + yc, x))

    def back_send(c):
        s, step = CHUNK_ORDER[c]
        source = lax.rem(z + NZ - step, NZ)
        if step != 0:
            wait_for(back.at[s, source], bz_r.at[c])
        place = s * NZ * NY + yc * NZ + source
        for d in Y_STEPS:
            yp = y_peer(d)
            send(back.at[s, source, yp], home.at[place], by_s.at[0], by_r.at[0], (z * NY + yp, x))
        pltpu.make_async_copy(back.at[s, source, yc], home.at[place], home_sem.at[0]).start()

    def find_positions():
        table_loads[1].wait()
        total = jnp.zeros((1, LANES), jnp.int32)
        owner = lax.broadcasted_iota(jnp.int32, (NZ * NY, LANES), 0)
        block = lax.broadcasted_iota(jnp.int32, (NZ * NY, LANES), 1)
        slot = lax.rem(owner, NY) * NZ + lax.div(owner, NY)
        for s in range(2):
            row = table_v[pl.ds(s, 1), :]
            held = jnp.broadcast_to(row, (LANES, NZ * NY)).T
            hit = jnp.where(held == block, slot + s * NZ * NY, 0)
            total += jnp.sum(hit, axis=0, keepdims=True)
        positions[...] = jnp.minimum(total, 2 * NZ * NY - 1)
        for s in range(2):
            factor = jnp.where(table[s, f] >= 0, decay_rate, 1.0).astype(jnp.float32)
            keep[s] = jnp.full((8, LANES), factor, jnp.float32)
        table_stores[0].start()
        table_stores[1].start()

    table_stores = [
        pltpu.make_async_copy(positions, positions_out, local_sem.at[7]),
        pltpu.make_async_copy(keep, keep_out, local_sem.at[8]),
    ]

    rs_first(0)
    left_loads[0].wait()
    l_send(0)
    rs_second(0)
    rs_first(1)
    l_send(1)
    table_loads[0].wait()
    rs_final(0)
    z_send(0, 0)
    z_send(0, 1)
    rs_second(1)
    l_send(2)
    l_send(3)
    share_send()
    left_loads[1].wait()
    l_send(4)
    l_send(5)
    find_positions()
    l_relay(0)
    l_relay(1)
    rs_final(1)
    z_send(1, 0)
    y_send(0, 0)
    l_relay(2)
    l_relay(3)
    l_relay_m(4)
    l_relay_m(5)
    g_send(0, 0)
    l_send(6)
    l_send(7)
    y_send(0, 1)
    share_pick()
    z_send(2, 0)
    z_send(1, 1)
    z_send(2, 1)
    l_relay_p(4)
    l_relay_p(5)
    y_send(1, 0)
    l_relay(6)
    g_send(1, 0)
    l_send_m(8)
    l_relay(7)
    y_send(2, 0)
    g_send(2, 0)
    g_relay_p(0)
    g_relay_m(0)
    g_send(0, 1)
    y_send(1, 1)
    g_send(1, 1)
    y_send(2, 1)
    right_load.wait()
    g_done(0)
    g_send(2, 1)
    l_send_m(9)
    right_product(0)
    for c in range(0, 5):
        update_chunk(c)
    update_chunk(7)
    g_relay_m(1)
    l_send_m(10)
    g_relay_p(1)
    l_send_p(8)
    l_send_p(9)
    l_send_p(10)
    l_relay_m(8)
    l_send_m(11)
    left_statistic(0)
    l_relay_m(9)
    l_send_m(12)
    right_statistic(0)
    l_relay_m(10)
    l_send_m(13)
    g_done(1)
    right_product(1)
    update_chunk(5)
    update_chunk(6)
    l_relay_p(8)
    l_send_p(11)
    l_relay_m(11)
    l_send_m(14)
    left_statistic(1)
    l_relay_p(9)
    l_send_p(12)
    l_relay_p(10)
    l_send_p(13)
    update_chunk(8)
    update_chunk(9)
    l_relay_m(12)
    l_send_m(15)
    update_chunk(10)
    right_statistic(1)
    back_send(0)
    back_send(2)
    l_relay_p(11)
    l_send_p(14)
    update_chunk(11)
    l_relay_m(13)
    back_send(1)
    back_send(4)
    l_relay_p(12)
    l_send_p(15)
    l_relay_p(13)
    l_relay_m(14)
    back_send(3)
    update_chunk(12)
    l_relay_p(14)
    l_relay_m(15)
    back_send(7)
    l_relay_p(15)
    update_chunk(13)
    back_send(8)
    back_send(5)
    back_send(6)
    update_chunk(14)
    back_send(14)
    update_chunk(15)
    back_send(15)
    for c in range(9, 14):
        back_send(c)

    for k, ref in enumerate((relay_p, relay_m, near_p, near_m, far_p, far_m)):
        wait_for(ref, rs_s.at[k])
    wait_for(shares.at[0], share_sem.at[0])
    wait_for(picked.at[:, :, pl.ds(0, (NZ - 1) * NY)], z_s.at[0])
    wait_for(landed.at[:, :, :, pl.ds(0, NY - 1)], y_s.at[0])
    where = lanes(x, SHARE)
    for k in range(2):
        wait_for(G.at[:, :, :, :, where], g_s.at[k])
        wait_for(G.at[:, pl.ds(0, NZ // 2), :, :, lanes(x * 2, LANES)], g_s.at[2 + k])
        wait_for(L.at[:, :, :, where], l_s.at[k])
    passed = len(BACKWARD) * LANES // 2
    wait_for(L.at[0, :, pl.ds(0, LANES - passed // NZ), where], l_s.at[2])
    wait_for(L.at[:, pl.ds(0, NZ // 2 + len(BACKWARD) // 4), :, where], l_s.at[3])
    wait_for(gv, local_sem.at[4])
    for copy in table_stores:
        copy.wait()
    wait_for(U.at[:, pl.ds(0, NZ - 1)], bz_s.at[0])
    wait_for(home.at[pl.ds(0, 2 * NZ * (NY - 1))], by_r.at[0])
    wait_for(back.at[:, :, pl.ds(0, NY - 1)], by_s.at[0])
    wait_for(home.at[pl.ds(0, CHUNKS)], home_sem.at[0])


def exchange(table, grad, left, right):
    bf16 = jnp.bfloat16
    any_spec = pl.BlockSpec(memory_space=pl.ANY)
    hbm_spec = pl.BlockSpec(memory_space=pltpu.HBM)
    dma = pltpu.SemaphoreType.DMA
    half = (2, HALF, ROWS, LANES)
    return pl.pallas_call(
        kernel,
        name="shampoo_exchange",
        out_shape=(
            jax.ShapeDtypeStruct((2, BS, SHARE), bf16),
            jax.ShapeDtypeStruct((2, BS, SHARE), bf16),
            jax.ShapeDtypeStruct((2 * NZ * NY, ROWS, SHARE), bf16),
            jax.ShapeDtypeStruct((1, LANES), jnp.int32),
            jax.ShapeDtypeStruct((2, 8, LANES), jnp.float32),
        ),
        in_specs=[hbm_spec, hbm_spec, hbm_spec, hbm_spec],
        out_specs=(any_spec,) * 5,
        scratch_shapes=[
            pltpu.SMEM((2, NZ * NY), jnp.int32),
            pltpu.VMEM((2, NZ * NY), jnp.int32),
            pltpu.VMEM((1, LANES), jnp.int32),
            pltpu.VMEM((2, 8, LANES), jnp.float32),
            pltpu.VMEM((2 * NX, BLOCKS, ROWS, LANES), bf16),
            pltpu.VMEM(half, bf16),
            pltpu.VMEM(half, bf16),
            pltpu.VMEM(half, bf16),
            pltpu.VMEM(half, bf16),
            pltpu.VMEM(half, bf16),
            pltpu.VMEM(half, bf16),
            pltpu.VMEM((2, BLOCKS, ROWS, LANES), bf16),
            pltpu.VMEM((BLOCKS, ROWS, LANES), bf16),
            pltpu.VMEM((3, 2, NZ * NY, ROWS, LANES), bf16),
            pltpu.VMEM((3, 2, NZ, NY, ROWS, LANES), bf16),
            pltpu.VMEM((2, NZ, NY, ROWS, BS), bf16),
            pltpu.VMEM((2, NZ, LANES, BS), bf16),
            pltpu.VMEM((2, BS, SHARE), bf16),
            pltpu.VMEM((2, BS, SHARE), bf16),
            pltpu.VMEM((2, NZ, NY, ROWS, SHARE), bf16),
            pltpu.VMEM((2, NZ, NY, ROWS, SHARE), bf16),
            pltpu.VMEM((2, BS, SHARE), bf16),
            pltpu.VMEM((2, BS, SHARE), bf16),
            dma((9,)),
            dma((1,)),
            dma((2,)),
            dma((6,)),
            dma((2, 3)),
            dma((1,)),
            dma((3, 2)),
            dma((1,)),
            dma((3, 2)),
            dma((4,)),
            dma((2, 2, 3)),
            dma((4,)),
            dma((CHUNKS, 3)),
            dma((1,)),
            dma((CHUNKS,)),
            dma((1,)),
            dma((1,)),
        ],
        compiler_params=pltpu.CompilerParams(
            collective_id=0, has_side_effects=True, vmem_limit_bytes=50 * 1024 * 1024
        ),
        cost_estimate=pl.CostEstimate(
            flops=16 * BS * BS * SHARE, bytes_accessed=16 * BS * BS, transcendentals=0
        ),
    )(table, grad, left, right)


def finish_kernel(
    left_stat, right_stat, left_term, right_term, home, positions_in, keep,
    left_next, right_next, update_out,
    left_new, right_new, positions, sem,
):
    load = pltpu.make_async_copy(positions_in, positions, sem.at[0])
    load.start()
    copies = []

    def next_of(s, stat, term, new, out, part):
        rows = pl.ds(part * (BS // 2), BS // 2)
        new[s, rows] = keep[s][:1, :1] * stat[s, rows] + (1.0 - decay_rate) * f32(term[s, rows])
        copy = pltpu.make_async_copy(new.at[s, rows], out.at[s, rows], sem.at[2 + len(copies)])
        copy.start()
        copies.append(copy)

    next_of(0, left_stat, left_term, left_new, left_next, 0)
    next_of(0, left_stat, left_term, left_new, left_next, 1)
    load.wait()

    def place(b, carry):
        pltpu.make_async_copy(home.at[positions[0, b]], update_out.at[b], sem.at[1]).start()
        return carry

    lax.fori_loop(0, BLOCKS, place, 0, unroll=8)
    for part in range(2):
        next_of(0, right_stat, right_term, right_new, right_next, part)
    for part in range(2):
        next_of(1, left_stat, left_term, left_new, left_next, part)
    for part in range(2):
        next_of(1, right_stat, right_term, right_new, right_next, part)
    for copy in copies:
        copy.wait()
    wait_for(update_out, sem.at[1])


def finish(*operands):
    vmem_spec = pl.BlockSpec(memory_space=pltpu.VMEM)
    any_spec = pl.BlockSpec(memory_space=pl.ANY)
    stat_shape = jax.ShapeDtypeStruct((2, BS, SHARE), jnp.float32)
    return pl.pallas_call(
        finish_kernel,
        name="shampoo_finish",
        out_shape=(
            stat_shape, stat_shape, jax.ShapeDtypeStruct((BLOCKS, ROWS, SHARE), jnp.bfloat16)
        ),
        in_specs=[vmem_spec] * 4 + [any_spec] * 2 + [vmem_spec],
        out_specs=(any_spec,) * 3,
        scratch_shapes=[
            pltpu.VMEM((2, BS, SHARE), jnp.float32),
            pltpu.VMEM((2, BS, SHARE), jnp.float32),
            pltpu.SMEM((1, LANES), jnp.int32),
            pltpu.SemaphoreType.DMA((10,)),
        ],
        compiler_params=pltpu.CompilerParams(vmem_limit_bytes=24 * 1024 * 1024),
        cost_estimate=pl.CostEstimate(flops=4 * BS * BS, bytes_accessed=8 * BS * BS, transcendentals=0),
    )(*operands)


def on_device(partial_grad, owner_table, left_stat, right_stat, left_root, right_root):
    left_term, right_term, home, positions, keep = exchange(
        owner_table.T,
        partial_grad[0],
        left_root[0].reshape(2, NZ, LANES, SHARE),
        right_root[0],
    )

    left_next, right_next, update = finish(
        left_stat[0], right_stat[0], left_term, right_term, home, positions, keep
    )
    return left_next[None], right_next[None], update


def solution(mesh):
    return jax.shard_map(
        on_device,
        mesh=mesh,
        in_specs=(
            P("rep", None, "fsdp", None),
            P(),
            P("fsdp", None, None, "rep"),
            P("fsdp", None, None, "rep"),
            P("fsdp", None, None, "rep"),
            P("fsdp", None, None, "rep"),
        ),
        out_specs=(
            P("fsdp", None, None, "rep"),
            P("fsdp", None, None, "rep"),
            P(None, "fsdp", "rep"),
        ),
        check_vma=False,
    )
```

time: 110 us -> 108 us (0.982)
  Pallas kernels: 109 us -> 107 us
    pallas_call x1, Pallas kernels: 107 us -> 104 us  [exchange(): pl.pallas_call(kernel, name='shampoo_exchange', out_shape=(jax.ShapeDtype...]
where the time goes in v3:
time: 108 us
  Pallas kernels  107 us (99%)
    pallas_call x1, Pallas kernels, exchange(): pl.pallas_call(kernel, name='shampoo_exchange', out_shape=(jax.ShapeDtype...  104 us
    pallas_call x1, Pallas kernels, finish(): pl.pallas_call(finish_kernel, name='shampoo_finish', out_shape=(stat_shap...  2.64 us

profile of v3, /device:TPU:1, one launch (start us, length us, event | category | flops | bytes accessed | tf_op | source)
XLA Modules:
  0.0 108.3 jit_solution(15354138420632568178)
XLA Ops:
  0.6 0.0 copy-start.2
  0.6 0.7 copy-done.2
  1.3 0.0 copy-start
  1.3 0.0 copy-start.1
  1.3 104.3 %shampoo_exchange.1 = (bf16[2,1024,256]{2,1,0:T(8,128)(2,1)S(1)}, bf16[2,1024,256]{2,1,0:T(8,128)(2,1)S(1)}, bf16[128,16,256]{2,1,0:T(8,128)(2,1)S(1)}, s32[1,128]{1,0:T(1,128)S(1)}, f32[2,8,128]{2,1,0:T(8,128)S(1)}) custom-call(s32[2,64]{1,0:T(2,128)S(1)} %bitcast.10, bf16[64,16,1024]{2,1,0:T(8,128)(2,1)} %bitcast.11, bf16[2,8,128,256]{3,2,1,0:T(8,128)(2,1)} %bitcast.14, ...), custom_call_target="tpu_custom_call" | custom-call | flops 4294967296 | bytes 16777216 | tf_op jit(solution)/shard_map/shampoo_exchange/pallas_call | solution.py:460
  105.7 0.0 copy-done
  105.7 0.0 copy-done.1
  105.7 2.6 %shampoo_finish.1 = (f32[2,1024,256]{2,1,0:T(8,128)}, f32[2,1024,256]{2,1,0:T(8,128)}, bf16[64,16,256]{2,1,0:T(8,128)(2,1)}) custom-call(f32[2,1024,256]{2,1,0:T(8,128)S(1)} %bitcast.8, f32[2,1024,256]{2,1,0:T(8,128)S(1)} %bitcast.9, bf16[2,1024,256]{2,1,0:T(8,128)(2,1)S(1)} %get-tuple-element.11.left_term, ...), custom_call_target="tpu_custom_call" | custom-call | flops 4194304 | bytes 8388608 | tf_op jit(solution)/shard_map/shampoo_finish/pallas_call | solution.py:563
Async XLA Ops:
  0.6 0.7 copy-start.2
  1.3 104.4 %copy-start = (f32[1,2,1024,256]{3,2,1,0:T(8,128)S(1)}, f32[1,2,1024,256]{3,2,1,0:T(8,128)}, u32[]{:S(2)}) copy-start(f32[1,2,1024,256]{3,2,1,0:T(8,128)} %param.8) | copy-start | bytes 6291460
  1.3 104.4 %copy-start.1 = (f32[1,2,1024,256]{3,2,1,0:T(8,128)S(1)}, f32[1,2,1024,256]{3,2,1,0:T(8,128)}, u32[]{:S(2)}) copy-start(f32[1,2,1024,256]{3,2,1,0:T(8,128)} %param.9) | copy-start | bytes 6291460

commit v4 on v3

--- a/solution.py
+++ b/solution.py
@@ -346,10 +346,10 @@
     z_send(2, 1)
     l_relay_p(4)
     l_relay_p(5)
+    l_send(8)
     y_send(1, 0)
     l_relay(6)
     g_send(1, 0)
-    l_send_m(8)
     l_relay(7)
     y_send(2, 0)
     g_send(2, 0)
@@ -370,9 +370,9 @@
     g_relay_m(1)
     l_send_m(10)
     g_relay_p(1)
-    l_send_p(8)
     l_send_p(9)
     l_send_p(10)
+    l_send_p(11)
     l_relay_m(8)
     l_send_m(11)
     left_statistic(0)
@@ -385,31 +385,30 @@
     right_product(1)
     update_chunk(5)
     update_chunk(6)
+    back_send(0)
+    back_send(2)
     l_relay_p(8)
-    l_send_p(11)
+    l_send_p(12)
     l_relay_m(11)
     l_send_m(14)
     left_statistic(1)
     l_relay_p(9)
-    l_send_p(12)
+    l_send_p(13)
     l_relay_p(10)
-    l_send_p(13)
+    l_send_p(14)
     update_chunk(8)
     update_chunk(9)
     l_relay_m(12)
     l_send_m(15)
+    l_send_p(15)
     update_chunk(10)
+    back_send(1)
+    back_send(4)
     right_statistic(1)
-    back_send(0)
-    back_send(2)
     l_relay_p(11)
-    l_send_p(14)
     update_chunk(11)
     l_relay_m(13)
-    back_send(1)
-    back_send(4)
     l_relay_p(12)
-    l_send_p(15)
     l_relay_p(13)
     l_relay_m(14)
     back_send(3)
@@ -422,12 +421,15 @@
     back_send(8)
     back_send(5)
     back_send(6)
+    back_send(9)
     update_chunk(14)
     back_send(14)
+    back_send(10)
     update_chunk(15)
     back_send(15)
-    for c in range(9, 14):
-        back_send(c)
+    back_send(11)
+    back_send(12)
+    back_send(13)
 
     for k, ref in enumerate((relay_p, relay_m, near_p, near_m, far_p, far_m)):
         wait_for(ref, rs_s.at[k])
@@ -536,21 +538,21 @@
         copy.start()
         copies.append(copy)
 
-    next_of(0, left_stat, left_term, left_new, left_next, 0)
-    next_of(0, left_stat, left_term, left_new, left_next, 1)
-    load.wait()
-
-    def place(b, carry):
-        pltpu.make_async_copy(home.at[positions[0, b]], update_out.at[b], sem.at[1]).start()
-        return carry
-
-    lax.fori_loop(0, BLOCKS, place, 0, unroll=8)
-    for part in range(2):
-        next_of(0, right_stat, right_term, right_new, right_next, part)
-    for part in range(2):
-        next_of(1, left_stat, left_term, left_new, left_next, part)
-    for part in range(2):
-        next_of(1, right_stat, right_term, right_new, right_next, part)
+    sides = (
+        (left_stat, left_term, left_new, left_next),
+        (right_stat, right_term, right_new, right_next),
+    )
+    parts = [(s, side, part) for s in range(2) for side in sides for part in range(2)]
+    placed = 0
+    for k, (s, side, part) in enumerate(parts):
+        next_of(s, *side, part)
+        if k == 1:
+            load.wait()
+        if k >= 1:
+            upto = BLOCKS * k // (len(parts) - 1)
+            for b in range(placed, upto):
+                pltpu.make_async_copy(home.at[positions[0, b]], update_out.at[b], sem.at[1]).start()
+            placed = upto
     for copy in copies:
         copy.wait()
     wait_for(update_out, sem.at[1])

time: 108 us -> 108 us (level)
  no operation moved by 1% of the time
where the time goes in v4:
time: 108 us
  Pallas kernels  106 us (98%)
    pallas_call x1, Pallas kernels, exchange(): pl.pallas_call(kernel, name='shampoo_exchange', out_shape=(jax.ShapeDtype...  104 us
    pallas_call x1, Pallas kernels, finish(): pl.pallas_call(finish_kernel, name='shampoo_finish', out_shape=(stat_shap...  2.64 us

profile of v4, /device:TPU:1, one launch (start us, length us, event | category | flops | bytes accessed | tf_op | source)
XLA Modules:
  0.0 107.5 jit_solution(15970236402090133883)
XLA Ops:
  0.6 0.0 copy-start.2
  0.6 0.7 copy-done.2
  1.3 0.0 copy-start
  1.3 0.0 copy-start.1
  1.3 103.6 %shampoo_exchange.1 = (bf16[2,1024,256]{2,1,0:T(8,128)(2,1)S(1)}, bf16[2,1024,256]{2,1,0:T(8,128)(2,1)S(1)}, bf16[128,16,256]{2,1,0:T(8,128)(2,1)S(1)}, s32[1,128]{1,0:T(1,128)S(1)}, f32[2,8,128]{2,1,0:T(8,128)S(1)}) custom-call(s32[2,64]{1,0:T(2,128)S(1)} %bitcast.10, bf16[64,16,1024]{2,1,0:T(8,128)(2,1)} %bitcast.11, bf16[2,8,128,256]{3,2,1,0:T(8,128)(2,1)} %bitcast.14, ...), custom_call_target="tpu_custom_call" | custom-call | flops 4294967296 | bytes 16777216 | tf_op jit(solution)/shard_map/shampoo_exchange/pallas_call | solution.py:462
  104.9 0.0 copy-done
  104.9 0.0 copy-done.1
  104.9 2.6 %shampoo_finish.1 = (f32[2,1024,256]{2,1,0:T(8,128)}, f32[2,1024,256]{2,1,0:T(8,128)}, bf16[64,16,256]{2,1,0:T(8,128)(2,1)}) custom-call(f32[2,1024,256]{2,1,0:T(8,128)S(1)} %bitcast.8, f32[2,1024,256]{2,1,0:T(8,128)S(1)} %bitcast.9, bf16[2,1024,256]{2,1,0:T(8,128)(2,1)S(1)} %get-tuple-element.11.left_term, ...), custom_call_target="tpu_custom_call" | custom-call | flops 4194304 | bytes 8388608 | tf_op jit(solution)/shard_map/shampoo_finish/pallas_call | solution.py:565
Async XLA Ops:
  0.6 0.7 copy-start.2
  1.3 103.6 %copy-start = (f32[1,2,1024,256]{3,2,1,0:T(8,128)S(1)}, f32[1,2,1024,256]{3,2,1,0:T(8,128)}, u32[]{:S(2)}) copy-start(f32[1,2,1024,256]{3,2,1,0:T(8,128)} %param.8) | copy-start | bytes 6291460
  1.3 103.6 %copy-start.1 = (f32[1,2,1024,256]{3,2,1,0:T(8,128)S(1)}, f32[1,2,1024,256]{3,2,1,0:T(8,128)}, u32[]{:S(2)}) copy-start(f32[1,2,1024,256]{3,2,1,0:T(8,128)} %param.9) | copy-start | bytes 6291460

commit v5 on v4

--- a/solution.py
+++ b/solution.py
@@ -24,6 +24,8 @@
 )
 CHUNKS = len(CHUNK_ORDER)
 BACKWARD = (9, 10, 11, 12)
+TOGETHER = (0, 1, 2, 3, 4, 7)
+LATER = tuple(c for c in range(CHUNKS) if c not in TOGETHER)
 
 
 def lanes(index, width):
@@ -54,7 +56,7 @@
     left_out, right_out, home, positions_out, keep_out,
     table, table_v, positions, keep, gv, relay_p, relay_m, near_p, near_m, far_p, far_m, shares, copied,
     picked, landed, G, L, R, T, U, back, left_term, right_term,
-    local_sem, home_sem, share_sem, rs_s, rs_r, z_s, z_r, y_s, y_r, g_s, g_r, l_s, l_r, bz_s, bz_r, by_s, by_r,
+    local_sem, home_sem, passed_sem, share_sem, rs_s, rs_r, z_s, z_r, y_s, y_r, g_s, g_r, l_s, l_r, bz_s, bz_r, by_s, by_r,
 ):
     f = lax.axis_index("fsdp")
     x = lax.axis_index("rep")
@@ -215,19 +217,22 @@
         l_send_p(c)
         l_send_m(c)
 
+    def relayed(c):
+        return passed_sem.at[0 if c in TOGETHER else 1 + LATER.index(c)]
+
     def l_relay_p(c):
         s, zc = chunk(c)
         wait_for(L.at[s, zc, :, lanes(prv, SHARE)], l_r.at[c, 0])
         if c not in BACKWARD:
             part = L.at[s, zc, pl.ds(0, LANES // 2), lanes(prv, SHARE)]
-            send(part, part, l_s.at[2], l_r.at[c, 2], to_nxt)
+            send(part, part, l_s.at[2], relayed(c), to_nxt)
 
     def l_relay_m(c):
         s, zc = chunk(c)
         wait_for(L.at[s, zc, :, lanes(nxt, SHARE)], l_r.at[c, 1])
         first = 0 if c in BACKWARD else LANES // 2
         part = L.at[s, zc, pl.ds(first, LANES - first), lanes(nxt, SHARE)]
-        send(part, part, l_s.at[3], l_r.at[c, 2], to_prv)
+        send(part, part, l_s.at[3], relayed(c), to_prv)
 
     def l_relay(c):
         l_relay_p(c)
@@ -267,7 +272,8 @@
 
     def update_chunk(c):
         s, zc = chunk(c)
-        wait_for(L.at[s, zc, :, lanes(opp, SHARE)], l_r.at[c, 2])
+        if c not in TOGETHER:
+            wait_for(L.at[s, zc, :, lanes(opp, SHARE)], relayed(c))
         result = jnp.dot(L[s, zc], T[s], preferred_element_type=jnp.float32)
         U[s, zc] = result.astype(jnp.bfloat16).reshape(NY, ROWS, SHARE)
         if CHUNK_ORDER[c][1] == 0:
@@ -353,8 +359,8 @@
     l_relay(7)
     y_send(2, 0)
     g_send(2, 0)
+    g_relay_m(0)
     g_relay_p(0)
-    g_relay_m(0)
     g_send(0, 1)
     y_send(1, 1)
     g_send(1, 1)
@@ -364,6 +370,7 @@
     g_send(2, 1)
     l_send_m(9)
     right_product(0)
+    wait_for(L.at[0, pl.ds(0, len(TOGETHER)), :, lanes(opp, SHARE)], passed_sem.at[0])
     for c in range(0, 5):
         update_chunk(c)
     update_chunk(7)
@@ -415,16 +422,16 @@
     update_chunk(12)
     l_relay_p(14)
     l_relay_m(15)
+    l_relay_p(15)
     back_send(7)
-    l_relay_p(15)
-    update_chunk(13)
     back_send(8)
     back_send(5)
+    update_chunk(13)
     back_send(6)
     back_send(9)
+    back_send(10)
     update_chunk(14)
     back_send(14)
-    back_send(10)
     update_chunk(15)
     back_send(15)
     back_send(11)
@@ -497,6 +504,7 @@
             pltpu.VMEM((2, BS, SHARE), bf16),
             dma((9,)),
             dma((1,)),
+            dma((1 + len(LATER),)),
             dma((2,)),
             dma((6,)),
             dma((2, 3)),
@@ -507,7 +515,7 @@
             dma((4,)),
             dma((2, 2, 3)),
             dma((4,)),
-            dma((CHUNKS, 3)),
+            dma((CHUNKS, 2)),
             dma((1,)),
             dma((CHUNKS,)),
             dma((1,)),

time: 108 us -> 108 us (level)
  no operation moved by 1% of the time
where the time goes in v5:
time: 108 us; the launch traced here: 107 us
  Pallas kernels  106 us (98%)
    pallas_call x1, Pallas kernels, exchange(): pl.pallas_call(kernel, name='shampoo_exchange', out_shape=(jax.ShapeDtype...  104 us
    pallas_call x1, Pallas kernels, finish(): pl.pallas_call(finish_kernel, name='shampoo_finish', out_shape=(stat_shap...  2.64 us

profile of v5, /device:TPU:1, one launch (start us, length us, event | category | flops | bytes accessed | tf_op | source)
XLA Modules:
  0.0 107.5 jit_solution(9162565041020803510)
XLA Ops:
  0.6 0.0 copy-start.2
  0.6 0.7 copy-done.2
  1.3 0.0 copy-start
  1.3 0.0 copy-start.1
  1.3 103.5 %shampoo_exchange.1 = (bf16[2,1024,256]{2,1,0:T(8,128)(2,1)S(1)}, bf16[2,1024,256]{2,1,0:T(8,128)(2,1)S(1)}, bf16[128,16,256]{2,1,0:T(8,128)(2,1)S(1)}, s32[1,128]{1,0:T(1,128)S(1)}, f32[2,8,128]{2,1,0:T(8,128)S(1)}) custom-call(s32[2,64]{1,0:T(2,128)S(1)} %bitcast.10, bf16[64,16,1024]{2,1,0:T(8,128)(2,1)} %bitcast.11, bf16[2,8,128,256]{3,2,1,0:T(8,128)(2,1)} %bitcast.14, ...), custom_call_target="tpu_custom_call" | custom-call | flops 4294967296 | bytes 16777216 | tf_op jit(solution)/shard_map/shampoo_exchange/pallas_call | solution.py:469
  104.8 0.0 copy-done
  104.8 0.0 copy-done.1
  104.9 2.6 %shampoo_finish.1 = (f32[2,1024,256]{2,1,0:T(8,128)}, f32[2,1024,256]{2,1,0:T(8,128)}, bf16[64,16,256]{2,1,0:T(8,128)(2,1)}) custom-call(f32[2,1024,256]{2,1,0:T(8,128)S(1)} %bitcast.8, f32[2,1024,256]{2,1,0:T(8,128)S(1)} %bitcast.9, bf16[2,1024,256]{2,1,0:T(8,128)(2,1)S(1)} %get-tuple-element.11.left_term, ...), custom_call_target="tpu_custom_call" | custom-call | flops 4194304 | bytes 8388608 | tf_op jit(solution)/shard_map/shampoo_finish/pallas_call | solution.py:573
Async XLA Ops:
  0.6 0.7 copy-start.2
  1.3 103.5 %copy-start = (f32[1,2,1024,256]{3,2,1,0:T(8,128)S(1)}, f32[1,2,1024,256]{3,2,1,0:T(8,128)}, u32[]{:S(2)}) copy-start(f32[1,2,1024,256]{3,2,1,0:T(8,128)} %param.8) | copy-start | bytes 6291460
  1.3 103.5 %copy-start.1 = (f32[1,2,1024,256]{3,2,1,0:T(8,128)S(1)}, f32[1,2,1024,256]{3,2,1,0:T(8,128)}, u32[]{:S(2)}) copy-start(f32[1,2,1024,256]{3,2,1,0:T(8,128)} %param.9) | copy-start | bytes 6291460
